TPU v7x, 128 devices: a whole 4x4x4 slice. The times are simulated.
128 devices in a mesh: gx: 16 (over z, y), gy: 8 (over x, core).
Axes of the slice: x: 4, y: 4, z: 4, core: 2. Of those that a mesh axis runs over, the one named last changes fastest.
Arguments:
- velocity_u: float32 [4, 2560, 2048], P(None, 'gy', 'gx'), may hold values from -6 to 6
- velocity_v: float32 [4, 2560, 2048], P(None, 'gy', 'gx'), may hold values from -6 to 6
- tracer: float32 [4, 2560, 2048], P(None, 'gy', 'gx'), may hold values from -6 to 6
- pressure_old: float32 [2560, 2048], P('gy', 'gx'), may hold values from -6 to 6
- depth: float32 [2560, 2048], P('gy', 'gx'), may hold values from 0.5 to 2
- helm: float32 [2560, 2048], P('gy', 'gx'), may hold values from 0.05 to 0.5
- land_mask: int32 [2560, 2048], P('gy', 'gx'), may hold values from 0 to 1, as said below
- clinic_map: int32 [64, 16], replicated, may hold values from 0 to 1, as said below
- tropic_map: int32 [64, 16], replicated, may hold values from -1 to 95, as said below
Outputs:
- velocity_u_new: float32 [4, 2560, 2048], P(None, 'gy', 'gx')
- velocity_v_new: float32 [4, 2560, 2048], P(None, 'gy', 'gx')
- tracer_new: float32 [4, 2560, 2048], P(None, 'gy', 'gx')
- pressure: float32 [2560, 2048], P('gy', 'gx')
Inputs may be any that keep to these rules, and one draw needn't show every extreme that they name: `land_mask`: rows 0 and 2559 are land; every column of a block whose tropic_map entry is -1 is land; every other block has an ocean column. `clinic_map`: 1 exactly on the blocks whose tropic_map entry is not -1. `tropic_map`: A quarter of the blocks of every device's clinic domain are -1. Another value t places the block in slot t % 6 of the device with gx index t // 6 and the gy index of the device that holds the block's rows; no slot is named twice. The blocks of one device's clinic domain place at most 1 block on any one device, and this bound is reached; every device receives at most 6 blocks, and this bound is reached.
All inputs are finite; a program needn't handle non-finite values.
Results may differ from a plain program's by a relative error of at most 0.00026.
Values sent between devices are 32-bit elements; how exact they have to be, the bound alone decides.
A program may use at most 64 MiB of HBM per device.

v0:
```python
import jax
import jax.numpy as jnp
from jax import lax
from jax.sharding import Mesh
from jax.sharding import PartitionSpec as P

BX = 128
BY = 40
ITERS = 4
GX_GY = ("gx_0", "gx_1", "gy_0", "gy_1")
GY = ("gy_0", "gy_1")
GX = ("gx_0", "gx_1")


step_time = 0.2
viscosity = 0.5
diffusivity = 0.5
vertical = 0.5
gravity = 1.0


def one_axis_at_a_time(x, axes):
    for axis in axes:
        x = lax.psum(x, axis)
    return x


def padded_2(cells, sides, width):
    for axis, dim in sides:
        count = lax.axis_size(axis)
        head = lax.slice_in_dim(cells, 0, width, axis=dim)
        tail = lax.slice_in_dim(cells, cells.shape[dim] - width, cells.shape[dim], axis=dim)
        cells = jnp.concatenate(
            [
                lax.ppermute(tail, axis, [(i, (i + 1) % count) for i in range(count)]),
                cells,
                lax.ppermute(head, axis, [((i + 1) % count, i) for i in range(count)]),
            ],
            axis=dim,
        )
    return cells


def padded_3(x, sides, width):
    edges = {}
    for axis, dim in sides:
        size, length = (lax.axis_size(axis), x.shape[dim])
        up = [(i, (i + 1) % size) for i in range(size)]
        last = lax.slice_in_dim(x, length - width, length, axis=dim)
        first = lax.slice_in_dim(x, 0, width, axis=dim)
        edges[dim] = (
            lax.ppermute(last, axis, up),
            lax.ppermute(first, axis, [(b, a) for a, b in up]),
        )
    done = []
    for _, dim in sides:
        low, high = edges[dim]
        around = [(width, width) if d in done else (0, 0) for d in range(x.ndim)]
        x = jnp.concatenate([jnp.pad(low, around), x, jnp.pad(high, around)], axis=dim)
        done.append(dim)
    return x


def beside_all(padded):
    centre = padded[..., 1:-1, 1:-1]
    return (
        centre,
        padded[..., 1:-1, 2:],
        padded[..., 1:-1, :-2],
        padded[..., 2:, 1:-1],
        padded[..., :-2, 1:-1],
    )


def faces(depths):
    centre, east_v, west_v, north_v, south_v = beside_all(depths)
    return (
        jnp.minimum(centre, east_v),
        jnp.minimum(centre, west_v),
        jnp.minimum(centre, north_v),
        jnp.minimum(centre, south_v),
    )


def diffuse(padded, coeffs):
    centre, east_v, west_v, north_v, south_v = beside_all(padded)
    face_e, face_w, face_n, face_s = coeffs
    return (
        face_e * (east_v - centre)
        + face_w * (west_v - centre)
        + face_n * (north_v - centre)
        + face_s * (south_v - centre)
    )


def mixing(field):
    diff = field[1:] - field[:-1]
    zero = jnp.zeros_like(field[:1])
    return jnp.concatenate([diff, zero], 0) - jnp.concatenate([zero, diff], 0)


def pair_totals(residual, precond, image):
    return (
        one_axis_at_a_time(jnp.sum(residual * precond), GX_GY),
        one_axis_at_a_time(jnp.sum(precond * image), GX_GY),
    )


def conjugate(apply, rhs, start, diagonal):
    solution = start
    residual = rhs - apply(start)
    precond = residual / diagonal
    image = apply(precond)
    rz_now, curve = pair_totals(residual, precond, image)
    alpha = rz_now / curve
    direction = precond
    along = image
    for step in range(ITERS):
        solution = solution + alpha * direction
        residual = residual - alpha * along
        if step + 1 < ITERS:
            precond = residual / diagonal
            image = apply(precond)
            rz_next, curve = pair_totals(residual, precond, image)
            ratio = rz_next / rz_now
            alpha = rz_next / (curve - ratio * rz_next / alpha)
            direction = precond + ratio * direction
            along = image + ratio * along
            rz_now = rz_next
    return solution


def on_device(
    velocity_u, velocity_v, tracer, pressure_old, depth, helm, land_mask, clinic_map, tropic_map
):
    f32 = jnp.float32
    levels, rows, cols = velocity_u.shape
    width_y = lax.axis_size(GY)
    col_dev = lax.axis_index(GX)
    row_dev = lax.axis_index(GY)
    per_y = rows // BY
    per_x = cols // BX
    total_rows = rows * width_y
    my_tropic = lax.dynamic_slice(tropic_map, (row_dev * per_y, col_dev * per_x), (per_y, per_x))
    my_clinic = lax.dynamic_slice(clinic_map, (row_dev * per_y, col_dev * per_x), (per_y, per_x))

    def spread(blockwise):
        return jnp.broadcast_to(blockwise[:, None, :, None], (per_y, BY, per_x, BX)).reshape(
            rows, cols
        )

    ocean = land_mask.astype(f32)
    domain = spread((my_tropic >= 0).astype(f32))
    active = spread(my_clinic.astype(f32))
    solve_mask = ocean * domain
    wet = depth * solve_mask
    stacked = jnp.concatenate([velocity_u, velocity_v, tracer, wet[None]], 0)
    padded = padded_2(stacked, ((GX, 2), (GY, 1)), 2)
    u_pad = padded[:levels]
    v_pad = padded[levels : 2 * levels]
    wet_pad = padded[3 * levels]
    cycle_faces = faces(wet_pad)
    inner_faces = tuple((face[1:-1, 1:-1] for face in cycle_faces))
    latitude = ((row_dev * rows - 1 + jnp.arange(rows + 2)) % total_rows).astype(f32)
    coriolis = (0.2 + 0.6 * ((latitude + 0.5) / total_rows)).reshape(rows + 2, 1)
    u_cycle = u_pad[:, 1:-1, 1:-1]
    v_cycle = v_pad[:, 1:-1, 1:-1]
    u_star = u_cycle + step_time * (
        vertical * mixing(u_cycle) + viscosity * diffuse(u_pad, cycle_faces) + coriolis * v_cycle
    )
    v_star = v_cycle + step_time * (
        vertical * mixing(v_cycle) + viscosity * diffuse(v_pad, cycle_faces) - coriolis * u_cycle
    )
    tracer_pad = padded[2 * levels : 3 * levels, 1:-1, 1:-1]
    _, tracer_e, tracer_w, tracer_n, tracer_s = beside_all(tracer_pad)
    tracer_raw = tracer + step_time * (
        vertical * mixing(tracer)
        + diffusivity * diffuse(tracer_pad, inner_faces)
        - 0.5 * (velocity_u * (tracer_e - tracer_w) + velocity_v * (tracer_n - tracer_s))
    )
    thick = ((2 * jnp.arange(levels) + 1).astype(f32) / (levels * levels)).reshape(levels, 1, 1)
    wet_cycle = wet_pad[1:-1, 1:-1]
    east_flow = wet_cycle * jnp.sum(thick * u_star, 0)
    north_flow = wet_cycle * jnp.sum(thick * v_star, 0)
    forcing = solve_mask * (
        -(east_flow[1:-1, 1:-1] - east_flow[1:-1, :-2])
        - (north_flow[1:-1, 1:-1] - north_flow[:-2, 1:-1])
    )
    face_e, face_w, face_n, face_s = inner_faces
    diagonal = helm + face_e + face_w + face_n + face_s
    start = solve_mask * pressure_old

    def plane_pad(field):
        return padded_3(field, ((GX, 1), (GY, 0)), 1)

    def apply_plane(field):
        _, east_v, west_v, north_v, south_v = beside_all(plane_pad(field))
        return (
            diagonal * field
            - face_e * east_v
            - face_w * west_v
            - face_n * north_v
            - face_s * south_v
        )

    pressure = conjugate(apply_plane, forcing, start, diagonal)
    _, east_p, _, north_p, _ = beside_all(plane_pad(pressure))
    grad_x = east_p - pressure
    grad_y = north_p - pressure
    keep_mask = active * ocean
    u_new = keep_mask * (u_star[:, 1:-1, 1:-1] - gravity * grad_x) + (1.0 - active) * velocity_u
    v_new = keep_mask * (v_star[:, 1:-1, 1:-1] - gravity * grad_y) + (1.0 - active) * velocity_v
    t_new = keep_mask * tracer_raw + (1.0 - active) * tracer
    return (u_new, v_new, t_new, pressure)


def solution(mesh):
    split = Mesh(mesh.devices.reshape(4, 4, 4, 2), ("gx_0", "gx_1", "gy_0", "gy_1"))
    in_specs = (
        P(None, GY, GX),
        P(None, GY, GX),
        P(None, GY, GX),
        P(GY, GX),
        P(GY, GX),
        P(GY, GX),
        P(GY, GX),
        P(),
        P(),
    )
    out_specs = (P(None, GY, GX), P(None, GY, GX), P(None, GY, GX), P(GY, GX))
    return jax.shard_map(
        on_device, mesh=split, in_specs=in_specs, out_specs=out_specs, check_vma=False
    )
```

profile of v0, /device:TPU:1, one launch (start us, length us, event | category | flops | bytes accessed | tf_op | source)
XLA Modules:
  0.0 265.6 jit_solution(10132375841164672830)
XLA Ops:
  9.5 7.1 %collective-permute-start.1 = (f32[13,320,2]{1,2,0:T(2,128)S(1)}, f32[13,320,2]{1,2,0:T(2,128)S(1)}, u32[]{:S(2)}, u32[]{:S(2)}) collective-permute-start(f32[13,320,2]{1,2,0:T(2,128)S(1)} %get-tuple-element.73), channel_id=1, source_target_pairs={{8,0},{16,8},{24,16},{32,24},{40,32},{48,40},{56,48},{64,56},{72,6... | collective-permute-start | bytes 99848 | tf_op jit(solution)/shard_map/ppermute | solution.py:37
  17.2 4.8 %collective-permute-start.4 = (f32[320,1]{0,1:T(1,128)}, f32[320,1]{0,1:T(1,128)}, u32[]{:S(2)}, u32[]{:S(2)}) collective-permute-start(f32[320,1]{0,1:T(1,128)} %get-tuple-element.108), channel_id=1, source_target_pairs={{8,0},{16,8},{24,16},{32,24},{40,32},{48,40},{56,48},{64,56},{72,6... | collective-permute-start | bytes 3848 | tf_op jit(solution)/shard_map/ppermute | solution.py:53
  22.7 2.6 collective-permute-start.7
  26.6 2.3 copy.42
  35.3 2.0 copy.43
  37.4 2.3 pad_maximum_fusion
  40.9 8.3 %multiply_reduce_fusion.1 = (f32[322,130]{0,1:T(8,128)S(1)}, f32[322,130]{0,1:T(8,128)S(1)}, f32[4,322,130]{1,2,0:T(8,128)}, f32[4,322,130]{1,2,0:T(8,128)}) fusion(f32[4]{0:T(128)S(1)} %copy-done.28, f32[13,324,132]{1,2,0:T(8,128)S(1)} %pad_maximum_fusion, f32[322]{0:T(512)S(1)} %fusion.91, f32[13,320,2]{1,2,0:T(2,128)S(1)} %collective-permute-done.1, ...), kind=kLoop, calls=%fused_computation.40 | loop fusion | flops 10632440 | bytes 9592600 | tf_op jit(solution)/shard_map/reduce_sum | solution.py:183
  51.0 5.1 %collective-permute-start.8 = (f32[320,1]{0,1:T(1,128)S(1)}, f32[320,1]{0,1:T(1,128)S(1)}, u32[]{:S(2)}, u32[]{:S(2)}) collective-permute-start(f32[320,1]{0,1:T(1,128)S(1)} %get-tuple-element.104), channel_id=1, source_target_pairs={{8,0},{16,8},{24,16},{32,24},{40,32},{48,40},{56,48},{64,56},{72,6... | collective-permute-start | bytes 3848 | tf_op jit(solution)/shard_map/ppermute | solution.py:53
  63.6 6.6 %all-reduce.28 = (f32[]{:T(128)}, f32[]{:T(128)}) all-reduce(f32[]{:T(128)} %get-tuple-element.19, f32[]{:T(128)} %get-tuple-element.18), channel_id=1, replica_groups=mesh['gx_0'=4,'gx_1'=4,'gy_0'=4,'gy_1'=2] {'gx_0'}, use_global_device_ids=true, to_apply=%region_3.4 | all-reduce | flops 2 | bytes 16 | tf_op jit(solution)/shard_map/psum | solution.py:24
  70.2 11.9 %all-reduce.24 = (f32[]{:T(128)}, f32[]{:T(128)}) all-reduce(f32[]{:T(128)} %get-tuple-element.44, f32[]{:T(128)} %get-tuple-element.45), channel_id=1, replica_groups=mesh['gx_0'=4,'gx_1'=4,'gy_0'=4,'gy_1'=2] {'gx_1'}, use_global_device_ids=true, to_apply=%region_4.5 | all-reduce | flops 2 | bytes 16 | tf_op jit(solution)/shard_map/psum | solution.py:24
  82.1 11.7 %all-reduce.20 = (f32[]{:T(128)}, f32[]{:T(128)}) all-reduce(f32[]{:T(128)} %get-tuple-element.36, f32[]{:T(128)} %get-tuple-element.37), channel_id=1, replica_groups=mesh['gx_0'=4,'gx_1'=4,'gy_0'=4,'gy_1'=2] {'gy_0'}, use_global_device_ids=true, to_apply=%region_5.6 | all-reduce | flops 2 | bytes 16 | tf_op jit(solution)/shard_map/psum | solution.py:24
  93.8 6.0 %all-reduce.32 = (f32[]{:T(128)}, f32[]{:T(128)}) all-reduce(f32[]{:T(128)} %get-tuple-element.28, f32[]{:T(128)} %get-tuple-element.29), channel_id=1, replica_groups=mesh['gx_0'=4,'gx_1'=4,'gy_0'=4,'gy_1'=2] {'gy_1'}, use_global_device_ids=true, to_apply=%region_6.7 | all-reduce | flops 2 | bytes 16 | tf_op jit(solution)/shard_map/psum | solution.py:24
  103.9 2.5 collective-permute-start.15
  107.7 2.4 collective-permute-done.14
  110.1 3.0 %multiply_reduce_fusion.5 = (f32[]{:T(128)}, f32[]{:T(128)}, f32[320,128]{0,1:T(8,128)}) fusion(f32[320,128]{0,1:T(8,128)S(1)} %get-tuple-element.60, f32[320,128]{0,1:T(8,128)S(1)} %get-tuple-element.61, f32[320,1]{0,1:T(1,128)S(1)} %collective-permute-done.12, f32[320,1]{0,1:T(1,128)S(1)} %collective-permute-done.13, ...), kind=kLoop, calls=%fused_computation.190 | loop fusion | flops 1105918 | bytes 1314312 | tf_op jit(solution)/shard_map/reduce_sum | solution.py:105
  113.1 6.8 %all-reduce.27 = (f32[]{:T(128)}, f32[]{:T(128)}) all-reduce(f32[]{:T(128)} %get-tuple-element.17, f32[]{:T(128)} %get-tuple-element.16), channel_id=1, replica_groups=mesh['gx_0'=4,'gx_1'=4,'gy_0'=4,'gy_1'=2] {'gx_0'}, use_global_device_ids=true, to_apply=%region_13.14 | all-reduce | flops 2 | bytes 16 | tf_op jit(solution)/shard_map/psum | solution.py:24
  119.9 10.0 %all-reduce.23 = (f32[]{:T(128)}, f32[]{:T(128)}) all-reduce(f32[]{:T(128)} %get-tuple-element.42, f32[]{:T(128)} %get-tuple-element.43), channel_id=1, replica_groups=mesh['gx_0'=4,'gx_1'=4,'gy_0'=4,'gy_1'=2] {'gx_1'}, use_global_device_ids=true, to_apply=%region_14.15 | all-reduce | flops 2 | bytes 16 | tf_op jit(solution)/shard_map/psum | solution.py:24
  129.9 8.8 %all-reduce.19 = (f32[]{:T(128)}, f32[]{:T(128)}) all-reduce(f32[]{:T(128)} %get-tuple-element.34, f32[]{:T(128)} %get-tuple-element.35), channel_id=1, replica_groups=mesh['gx_0'=4,'gx_1'=4,'gy_0'=4,'gy_1'=2] {'gy_0'}, use_global_device_ids=true, to_apply=%region_15.16 | all-reduce | flops 2 | bytes 16 | tf_op jit(solution)/shard_map/psum | solution.py:24
  138.7 6.8 %all-reduce.31 = (f32[]{:T(128)}, f32[]{:T(128)}) all-reduce(f32[]{:T(128)} %get-tuple-element.26, f32[]{:T(128)} %get-tuple-element.27), channel_id=1, replica_groups=mesh['gx_0'=4,'gx_1'=4,'gy_0'=4,'gy_1'=2] {'gy_1'}, use_global_device_ids=true, to_apply=%region_16.17 | all-reduce | flops 2 | bytes 16 | tf_op jit(solution)/shard_map/psum | solution.py:24
  155.9 2.7 collective-permute-done.18
  160.3 6.7 %all-reduce.26 = (f32[]{:T(128)}, f32[]{:T(128)}) all-reduce(f32[]{:T(128)} %get-tuple-element.15, f32[]{:T(128)} %get-tuple-element.14), channel_id=1, replica_groups=mesh['gx_0'=4,'gx_1'=4,'gy_0'=4,'gy_1'=2] {'gx_0'}, use_global_device_ids=true, to_apply=%region_23.24 | all-reduce | flops 2 | bytes 16 | tf_op jit(solution)/shard_map/psum | solution.py:24
  167.0 10.0 %all-reduce.22 = (f32[]{:T(128)}, f32[]{:T(128)}) all-reduce(f32[]{:T(128)} %get-tuple-element.40, f32[]{:T(128)} %get-tuple-element.41), channel_id=1, replica_groups=mesh['gx_0'=4,'gx_1'=4,'gy_0'=4,'gy_1'=2] {'gx_1'}, use_global_device_ids=true, to_apply=%region_24.25 | all-reduce | flops 2 | bytes 16 | tf_op jit(solution)/shard_map/psum | solution.py:24
  177.0 10.1 %all-reduce.18 = (f32[]{:T(128)}, f32[]{:T(128)}) all-reduce(f32[]{:T(128)} %get-tuple-element.32, f32[]{:T(128)} %get-tuple-element.33), channel_id=1, replica_groups=mesh['gx_0'=4,'gx_1'=4,'gy_0'=4,'gy_1'=2] {'gy_0'}, use_global_device_ids=true, to_apply=%region_25.26 | all-reduce | flops 2 | bytes 16 | tf_op jit(solution)/shard_map/psum | solution.py:24
  187.1 5.7 %all-reduce.30 = (f32[]{:T(128)}, f32[]{:T(128)}) all-reduce(f32[]{:T(128)} %get-tuple-element.24, f32[]{:T(128)} %get-tuple-element.25), channel_id=1, replica_groups=mesh['gx_0'=4,'gx_1'=4,'gy_0'=4,'gy_1'=2] {'gy_1'}, use_global_device_ids=true, to_apply=%region_26.27 | all-reduce | flops 2 | bytes 16 | tf_op jit(solution)/shard_map/psum | solution.py:24
  208.8 6.6 %all-reduce.25 = (f32[]{:T(128)}, f32[]{:T(128)}) all-reduce(f32[]{:T(128)} %get-tuple-element.13, f32[]{:T(128)} %get-tuple-element.12), channel_id=1, replica_groups=mesh['gx_0'=4,'gx_1'=4,'gy_0'=4,'gy_1'=2] {'gx_0'}, use_global_device_ids=true, to_apply=%region_33.34 | all-reduce | flops 2 | bytes 16 | tf_op jit(solution)/shard_map/psum | solution.py:24
  215.4 10.4 %all-reduce.21 = (f32[]{:T(128)}, f32[]{:T(128)}) all-reduce(f32[]{:T(128)} %get-tuple-element.38, f32[]{:T(128)} %get-tuple-element.39), channel_id=1, replica_groups=mesh['gx_0'=4,'gx_1'=4,'gy_0'=4,'gy_1'=2] {'gx_1'}, use_global_device_ids=true, to_apply=%region_34.35 | all-reduce | flops 2 | bytes 16 | tf_op jit(solution)/shard_map/psum | solution.py:24
  225.8 7.4 %all-reduce.17 = (f32[]{:T(128)}, f32[]{:T(128)}) all-reduce(f32[]{:T(128)} %get-tuple-element.30, f32[]{:T(128)} %get-tuple-element.31), channel_id=1, replica_groups=mesh['gx_0'=4,'gx_1'=4,'gy_0'=4,'gy_1'=2] {'gy_0'}, use_global_device_ids=true, to_apply=%region_35.36 | all-reduce | flops 2 | bytes 16 | tf_op jit(solution)/shard_map/psum | solution.py:24
  233.1 9.7 %all-reduce.29 = (f32[]{:T(128)}, f32[]{:T(128)}) all-reduce(f32[]{:T(128)} %get-tuple-element.22, f32[]{:T(128)} %get-tuple-element.23), channel_id=1, replica_groups=mesh['gx_0'=4,'gx_1'=4,'gy_0'=4,'gy_1'=2] {'gy_1'}, use_global_device_ids=true, to_apply=%region_36.37 | all-reduce | flops 2 | bytes 16 | tf_op jit(solution)/shard_map/psum | solution.py:24
  251.2 4.4 %multiply_add_fusion = f32[4,320,128]{1,2,0:T(8,128)} fusion(f32[4,320,128]{1,2,0:T(8,128)S(1)} %copy.40, f32[4,320,128]{1,2,0:T(8,128)S(1)} %copy.39, f32[4,320,128]{1,2,0:T(8,128)S(1)} %copy.38, f32[13,320,2]{1,2,0:T(2,128)S(1)} %collective-permute-done.1, f32[1,320,128]{1,2,0:T(8,128)} %copy-done.13, f32[13,320,2]{1,2,0:T(2,128)S(1)} %collective-permute-done, ...), kind=kLoop, calls=%fused_computation.67 | loop fusion | flops 7536640 | bytes 4191296 | tf_op jit(solution)/shard_map/add | solution.py:213
  255.5 2.3 copy.63
  259.7 2.6 fusion.25
  262.3 2.2 copy.61
  (158 shorter events, 59.0 us)
Async XLA Ops:
  9.5 31.3 %copy-start.13 = (f32[1,320,128]{1,2,0:T(8,128)}, f32[1,320,128]{1,2,0:T(8,128)S(1)}, u32[]{:S(2)}) copy-start(f32[1,320,128]{1,2,0:T(8,128)S(1)} %get-tuple-element.83) | copy-start | bytes 491524
  9.5 15.8 %collective-permute-start.1 = (f32[13,320,2]{1,2,0:T(2,128)S(1)}, f32[13,320,2]{1,2,0:T(2,128)S(1)}, u32[]{:S(2)}, u32[]{:S(2)}) collective-permute-start(f32[13,320,2]{1,2,0:T(2,128)S(1)} %get-tuple-element.73), channel_id=1, source_target_pairs={{8,0},{16,8},{24,16},{32,24},{40,32},{48,40},{56,48},{64,56},{72,6... | collective-permute-start | bytes 99848 | tf_op jit(solution)/shard_map/ppermute | solution.py:37
  16.6 8.7 %collective-permute-start = (f32[13,320,2]{1,2,0:T(2,128)S(1)}, f32[13,320,2]{1,2,0:T(2,128)S(1)}, u32[]{:S(2)}, u32[]{:S(2)}) collective-permute-start(f32[13,320,2]{1,2,0:T(2,128)S(1)} %get-tuple-element.72), channel_id=1, source_target_pairs={{0,8},{8,16},{16,24},{24,32},{32,40},{40,48},{48,56},{56,64},{64,7... | collective-permute-start | bytes 99848 | tf_op jit(solution)/shard_map/ppermute | solution.py:35
  17.2 32.2 %collective-permute-start.4 = (f32[320,1]{0,1:T(1,128)}, f32[320,1]{0,1:T(1,128)}, u32[]{:S(2)}, u32[]{:S(2)}) collective-permute-start(f32[320,1]{0,1:T(1,128)} %get-tuple-element.108), channel_id=1, source_target_pairs={{8,0},{16,8},{24,16},{32,24},{40,32},{48,40},{56,48},{64,56},{72,6... | collective-permute-start | bytes 3848 | tf_op jit(solution)/shard_map/ppermute | solution.py:53
  22.0 27.4 %collective-permute-start.5 = (f32[320,1]{0,1:T(1,128)}, f32[320,1]{0,1:T(1,128)}, u32[]{:S(2)}, u32[]{:S(2)}) collective-permute-start(f32[320,1]{0,1:T(1,128)} %get-tuple-element.107), channel_id=1, source_target_pairs={{0,8},{8,16},{16,24},{24,32},{32,40},{40,48},{48,56},{56,64},{64,7... | collective-permute-start | bytes 3848 | tf_op jit(solution)/shard_map/ppermute | solution.py:52
  22.7 26.6 %collective-permute-start.7 = (f32[1,128]{0,1:T(8,128)}, f32[1,128]{0,1:T(8,128)}, u32[]{:S(2)}, u32[]{:S(2)}) collective-permute-start(f32[1,128]{0,1:T(8,128)} %get-tuple-element.106), channel_id=1, source_target_pairs={{0,1},{1,2},{2,3},{3,4},{4,5},{5,6},{6,7},{7,0},{8,9},{9,10},{10,1... | collective-permute-start | bytes 1544 | tf_op jit(solution)/shard_map/ppermute | solution.py:52
  28.9 5.2 %collective-permute-start.3 = (f32[13,2,132]{2,1,0:T(2,128)}, f32[13,2,132]{2,1,0:T(2,128)}, u32[]{:S(2)}, u32[]{:S(2)}) collective-permute-start(f32[13,2,132]{2,1,0:T(2,128)} %copy.42), channel_id=1, source_target_pairs={{1,0},{2,1},{3,2},{4,3},{5,4},{6,5},{7,6},{0,7},{9,8},{10,9},{11,1... | collective-permute-start | bytes 41192 | tf_op jit(solution)/shard_map/ppermute | solution.py:37
  30.0 5.3 %collective-permute-start.2 = (f32[13,2,132]{2,1,0:T(2,128)}, f32[13,2,132]{2,1,0:T(2,128)}, u32[]{:S(2)}, u32[]{:S(2)}) collective-permute-start(f32[13,2,132]{2,1,0:T(2,128)} %copy.41), channel_id=1, source_target_pairs={{0,1},{1,2},{2,3},{3,4},{4,5},{5,6},{6,7},{7,0},{8,9},{9,10},{10,1... | collective-permute-start | bytes 41192 | tf_op jit(solution)/shard_map/ppermute | solution.py:35
  34.1 15.3 %collective-permute-start.6 = (f32[1,128]{0,1:T(8,128)}, f32[1,128]{0,1:T(8,128)}, u32[]{:S(2)}, u32[]{:S(2)}) collective-permute-start(f32[1,128]{0,1:T(8,128)} %get-tuple-element.105), channel_id=1, source_target_pairs={{1,0},{2,1},{3,2},{4,3},{5,4},{6,5},{7,6},{0,7},{9,8},{10,9},{11,1... | collective-permute-start | bytes 1544 | tf_op jit(solution)/shard_map/ppermute | solution.py:53
  40.8 21.1 %copy-start.1 = (f32[322,130]{0,1:T(8,128)}, f32[322,130]{0,1:T(8,128)S(1)}, u32[]{:S(2)}) copy-start(f32[322,130]{0,1:T(8,128)S(1)} %get-tuple-element.76) | copy-start | bytes 502324
  40.8 21.0 %copy-start.4 = (f32[322,130]{0,1:T(8,128)}, f32[322,130]{0,1:T(8,128)S(1)}, u32[]{:S(2)}) copy-start(f32[322,130]{0,1:T(8,128)S(1)} %get-tuple-element.77) | copy-start | bytes 502324
  40.8 21.0 %copy-start.7 = (f32[322,130]{0,1:T(8,128)}, f32[322,130]{0,1:T(8,128)S(1)}, u32[]{:S(2)}) copy-start(f32[322,130]{0,1:T(8,128)S(1)} %get-tuple-element.78) | copy-start | bytes 502324
  40.8 21.0 %copy-start.10 = (f32[322,130]{0,1:T(8,128)}, f32[322,130]{0,1:T(8,128)S(1)}, u32[]{:S(2)}) copy-start(f32[322,130]{0,1:T(8,128)S(1)} %get-tuple-element.79) | copy-start | bytes 502324
  51.0 10.8 %collective-permute-start.8 = (f32[320,1]{0,1:T(1,128)S(1)}, f32[320,1]{0,1:T(1,128)S(1)}, u32[]{:S(2)}, u32[]{:S(2)}) collective-permute-start(f32[320,1]{0,1:T(1,128)S(1)} %get-tuple-element.104), channel_id=1, source_target_pairs={{8,0},{16,8},{24,16},{32,24},{40,32},{48,40},{56,48},{64,56},{72,6... | collective-permute-start | bytes 3848 | tf_op jit(solution)/shard_map/ppermute | solution.py:53
  56.1 5.8 %collective-permute-start.9 = (f32[320,1]{0,1:T(1,128)S(1)}, f32[320,1]{0,1:T(1,128)S(1)}, u32[]{:S(2)}, u32[]{:S(2)}) collective-permute-start(f32[320,1]{0,1:T(1,128)S(1)} %get-tuple-element.103), channel_id=1, source_target_pairs={{0,8},{8,16},{16,24},{24,32},{32,40},{40,48},{48,56},{56,64},{64,7... | collective-permute-start | bytes 3848 | tf_op jit(solution)/shard_map/ppermute | solution.py:52
  56.2 4.0 %collective-permute-start.11 = (f32[1,128]{0,1:T(8,128)S(1)}, f32[1,128]{0,1:T(8,128)S(1)}, u32[]{:S(2)}, u32[]{:S(2)}) collective-permute-start(f32[1,128]{0,1:T(8,128)S(1)} %get-tuple-element.102), channel_id=1, source_target_pairs={{0,1},{1,2},{2,3},{3,4},{4,5},{5,6},{6,7},{7,0},{8,9},{9,10},{10,1... | collective-permute-start | bytes 1544 | tf_op jit(solution)/shard_map/ppermute | solution.py:52
  58.1 3.7 %collective-permute-start.10 = (f32[1,128]{0,1:T(8,128)S(1)}, f32[1,128]{0,1:T(8,128)S(1)}, u32[]{:S(2)}, u32[]{:S(2)}) collective-permute-start(f32[1,128]{0,1:T(8,128)S(1)} %get-tuple-element.101), channel_id=1, source_target_pairs={{1,0},{2,1},{3,2},{4,3},{5,4},{6,5},{7,6},{0,7},{9,8},{10,9},{11,1... | collective-permute-start | bytes 1544 | tf_op jit(solution)/shard_map/ppermute | solution.py:53
  102.2 7.8 %collective-permute-start.12 = (f32[320,1]{0,1:T(1,128)S(1)}, f32[320,1]{0,1:T(1,128)S(1)}, u32[]{:S(2)}, u32[]{:S(2)}) collective-permute-start(f32[320,1]{0,1:T(1,128)S(1)} %get-tuple-element.100), channel_id=1, source_target_pairs={{8,0},{16,8},{24,16},{32,24},{40,32},{48,40},{56,48},{64,56},{72,6... | collective-permute-start | bytes 3848 | tf_op jit(solution)/shard_map/ppermute | solution.py:53
  102.3 7.8 %collective-permute-start.13 = (f32[320,1]{0,1:T(1,128)S(1)}, f32[320,1]{0,1:T(1,128)S(1)}, u32[]{:S(2)}, u32[]{:S(2)}) collective-permute-start(f32[320,1]{0,1:T(1,128)S(1)} %get-tuple-element.99), channel_id=1, source_target_pairs={{0,8},{8,16},{16,24},{24,32},{32,40},{40,48},{48,56},{56,64},{64,7... | collective-permute-start | bytes 3848 | tf_op jit(solution)/shard_map/ppermute | solution.py:52
  103.9 3.9 %collective-permute-start.15 = (f32[1,128]{0,1:T(8,128)S(1)}, f32[1,128]{0,1:T(8,128)S(1)}, u32[]{:S(2)}, u32[]{:S(2)}) collective-permute-start(f32[1,128]{0,1:T(8,128)S(1)} %get-tuple-element.98), channel_id=1, source_target_pairs={{0,1},{1,2},{2,3},{3,4},{4,5},{5,6},{6,7},{7,0},{8,9},{9,10},{10,1... | collective-permute-start | bytes 1544 | tf_op jit(solution)/shard_map/ppermute | solution.py:52
  106.4 3.7 %collective-permute-start.14 = (f32[1,128]{0,1:T(8,128)S(1)}, f32[1,128]{0,1:T(8,128)S(1)}, u32[]{:S(2)}, u32[]{:S(2)}) collective-permute-start(f32[1,128]{0,1:T(8,128)S(1)} %get-tuple-element.97), channel_id=1, source_target_pairs={{1,0},{2,1},{3,2},{4,3},{5,4},{6,5},{7,6},{0,7},{9,8},{10,9},{11,1... | collective-permute-start | bytes 1544 | tf_op jit(solution)/shard_map/ppermute | solution.py:53
  151.3 7.2 %collective-permute-start.16 = (f32[320,1]{0,1:T(1,128)S(1)}, f32[320,1]{0,1:T(1,128)S(1)}, u32[]{:S(2)}, u32[]{:S(2)}) collective-permute-start(f32[320,1]{0,1:T(1,128)S(1)} %get-tuple-element.96), channel_id=1, source_target_pairs={{8,0},{16,8},{24,16},{32,24},{40,32},{48,40},{56,48},{64,56},{72,6... | collective-permute-start | bytes 3848 | tf_op jit(solution)/shard_map/ppermute | solution.py:53
  151.7 6.8 %collective-permute-start.17 = (f32[320,1]{0,1:T(1,128)S(1)}, f32[320,1]{0,1:T(1,128)S(1)}, u32[]{:S(2)}, u32[]{:S(2)}) collective-permute-start(f32[320,1]{0,1:T(1,128)S(1)} %get-tuple-element.95), channel_id=1, source_target_pairs={{0,8},{8,16},{16,24},{24,32},{32,40},{40,48},{48,56},{56,64},{64,7... | collective-permute-start | bytes 3848 | tf_op jit(solution)/shard_map/ppermute | solution.py:52
  152.8 3.1 %collective-permute-start.19 = (f32[1,128]{0,1:T(8,128)S(1)}, f32[1,128]{0,1:T(8,128)S(1)}, u32[]{:S(2)}, u32[]{:S(2)}) collective-permute-start(f32[1,128]{0,1:T(8,128)S(1)} %get-tuple-element.94), channel_id=1, source_target_pairs={{0,1},{1,2},{2,3},{3,4},{4,5},{5,6},{6,7},{7,0},{8,9},{9,10},{10,1... | collective-permute-start | bytes 1544 | tf_op jit(solution)/shard_map/ppermute | solution.py:52
  154.5 4.0 %collective-permute-start.18 = (f32[1,128]{0,1:T(8,128)S(1)}, f32[1,128]{0,1:T(8,128)S(1)}, u32[]{:S(2)}, u32[]{:S(2)}) collective-permute-start(f32[1,128]{0,1:T(8,128)S(1)} %get-tuple-element.93), channel_id=1, source_target_pairs={{1,0},{2,1},{3,2},{4,3},{5,4},{6,5},{7,6},{0,7},{9,8},{10,9},{11,1... | collective-permute-start | bytes 1544 | tf_op jit(solution)/shard_map/ppermute | solution.py:53
  198.2 9.5 %collective-permute-start.23 = (f32[1,128]{0,1:T(8,128)S(1)}, f32[1,128]{0,1:T(8,128)S(1)}, u32[]{:S(2)}, u32[]{:S(2)}) collective-permute-start(f32[1,128]{0,1:T(8,128)S(1)} %get-tuple-element.90), channel_id=1, source_target_pairs={{0,1},{1,2},{2,3},{3,4},{4,5},{5,6},{6,7},{7,0},{8,9},{9,10},{10,1... | collective-permute-start | bytes 1544 | tf_op jit(solution)/shard_map/ppermute | solution.py:52
  200.2 7.5 %collective-permute-start.20 = (f32[320,1]{0,1:T(1,128)S(1)}, f32[320,1]{0,1:T(1,128)S(1)}, u32[]{:S(2)}, u32[]{:S(2)}) collective-permute-start(f32[320,1]{0,1:T(1,128)S(1)} %get-tuple-element.92), channel_id=1, source_target_pairs={{8,0},{16,8},{24,16},{32,24},{40,32},{48,40},{56,48},{64,56},{72,6... | collective-permute-start | bytes 3848 | tf_op jit(solution)/shard_map/ppermute | solution.py:53
  200.2 7.5 %collective-permute-start.21 = (f32[320,1]{0,1:T(1,128)S(1)}, f32[320,1]{0,1:T(1,128)S(1)}, u32[]{:S(2)}, u32[]{:S(2)}) collective-permute-start(f32[320,1]{0,1:T(1,128)S(1)} %get-tuple-element.91), channel_id=1, source_target_pairs={{0,8},{8,16},{16,24},{24,32},{32,40},{40,48},{48,56},{56,64},{64,7... | collective-permute-start | bytes 3848 | tf_op jit(solution)/shard_map/ppermute | solution.py:52
  201.7 6.0 %collective-permute-start.22 = (f32[1,128]{0,1:T(8,128)S(1)}, f32[1,128]{0,1:T(8,128)S(1)}, u32[]{:S(2)}, u32[]{:S(2)}) collective-permute-start(f32[1,128]{0,1:T(8,128)S(1)} %get-tuple-element.89), channel_id=1, source_target_pairs={{1,0},{2,1},{3,2},{4,3},{5,4},{6,5},{7,6},{0,7},{9,8},{10,9},{11,1... | collective-permute-start | bytes 1544 | tf_op jit(solution)/shard_map/ppermute | solution.py:53
  249.4 9.3 %collective-permute-start.26 = (f32[1,128]{0,1:T(8,128)}, f32[1,128]{0,1:T(8,128)}, u32[]{:S(2)}, u32[]{:S(2)}) collective-permute-start(f32[1,128]{0,1:T(8,128)} %slice.452), channel_id=1, source_target_pairs={{1,0},{2,1},{3,2},{4,3},{5,4},{6,5},{7,6},{0,7},{9,8},{10,9},{11,1... | collective-permute-start | bytes 1544 | tf_op jit(solution)/shard_map/ppermute | solution.py:53
  249.7 8.9 %collective-permute-start.24 = (f32[320,1]{0,1:T(1,128)}, f32[320,1]{0,1:T(1,128)S(1)}, u32[]{:S(2)}, u32[]{:S(2)}) collective-permute-start(f32[320,1]{0,1:T(1,128)} %get-tuple-element.87), channel_id=1, source_target_pairs={{8,0},{16,8},{24,16},{32,24},{40,32},{48,40},{56,48},{64,56},{72,6... | collective-permute-start | bytes 3848 | tf_op jit(solution)/shard_map/ppermute | solution.py:53
  249.7 8.9 %collective-permute-start.25 = (f32[320,1]{0,1:T(1,128)}, f32[320,1]{0,1:T(1,128)S(1)}, u32[]{:S(2)}, u32[]{:S(2)}) collective-permute-start(f32[320,1]{0,1:T(1,128)} %get-tuple-element.86), channel_id=1, source_target_pairs={{0,8},{8,16},{16,24},{24,32},{32,40},{40,48},{48,56},{56,64},{64,7... | collective-permute-start | bytes 3848 | tf_op jit(solution)/shard_map/ppermute | solution.py:52
  (24 other events, 208.3 us)
where the time goes:
time: 267 us; the launch traced here: 266 us
  blocking collectives  135 us (51%)
  other arithmetic  38.9 us (15%)
  starting transfers between devices  37.3 us (14%)
  local copies, waits for them, and re-layouts  30.2 us (11%)
  between operations  14.8 us (6%)
  waiting for transfers between devices  9.27 us (3%)
    psum x16, blocking collectives, one_axis_at_a_time(): x = lax.psum(x, axis)  135 us
    ppermute x11, starting transfers between devices, padded_3(): lax.ppermute(last, axis, up)  16.2 us
    unnamed x69, local copies, waits for them, and re-layouts  14.5 us
    ppermute x12, starting transfers between devices, padded_3(): lax.ppermute(first, axis, [(b, a) for a, b in up])  12.2 us
    reduce_sum x1, other arithmetic, on_device(): east_flow = wet_cycle * jnp.sum(thick * u_star, 0)  8.32 us
    reduce_sum x4, other arithmetic, pair_totals(): jnp.sum(precond * image)  7.51 us
    ppermute x2, starting transfers between devices, padded_2(): lax.ppermute(head, axis, [((i + 1) % count, i) for i in range(count)])  7.1 us
    ppermute x12, waiting for transfers between devices, padded_3(): lax.ppermute(first, axis, [(b, a) for a, b in up])  6.65 us
  transfers between devices with their start and end apart: 27, of which 7 were waited for; matrix products, arithmetic and copies ran while one was open for 14% of the time, Pallas kernels for 0%

commit v1 on v0

v1 whole, which is shorter than its diff:
```python
import functools

import jax
import jax.numpy as jnp
from jax import lax
from jax.experimental import pallas as pl
from jax.experimental.pallas import tpu as pltpu
from jax.sharding import PartitionSpec as P

MESH = pl.DeviceIdType.MESH
F32 = jnp.float32

LEVELS, ROWS, COLS, BY, NY = 4, 320, 128, 40, 2560
BLOCKS, NBY = ROWS // BY, 64
THICK = [(2 * k + 1) / (LEVELS * LEVELS) for k in range(LEVELS)]

OFF = 16
EXT_ROWS = ROWS + 2 * OFF
LOW, HIGH = OFF - 8, OFF + ROWS + 8
STEP = 48
FIELDS = 7
WET, HELM, X0, UB, UH, VB, VH = range(FIELDS)
PLANES = 3 * LEVELS
NX_DEV, NY_DEV = 16, 8

VMEM_LIMIT = 54 * 1024 * 1024
RED_STAGES = ("all",)


def peers(kind):
    gx, gy = lax.axis_index("gx"), lax.axis_index("gy")
    if kind == "halo":
        return [
            (lax.rem(gx + i, NX_DEV), lax.rem(gy + j, NY_DEV))
            for i in (0, 1, NX_DEV - 1)
            for j in (0, 1, NY_DEV - 1)
            if i or j
        ]
    if kind == "plane":
        base = gx // 4 * 4
        return [
            (base + lax.rem(lax.rem(gx, 4) + i, 4), lax.rem(gy + j, NY_DEV))
            for i in range(4)
            for j in range(NY_DEV)
            if i or j
        ]
    if kind == "z":
        return [(lax.rem(gx + 4 * j, NX_DEV), gy) for j in range(1, 4)]
    return [
        (lax.rem(gx + i, NX_DEV), lax.rem(gy + j, NY_DEV))
        for i in range(NX_DEV)
        for j in range(NY_DEV)
        if i or j
    ]


COUNT = {"all": 127, "plane": 31, "z": 3}


def lanes(rows):
    return lax.broadcasted_iota(jnp.int32, (rows, COLS), 1)


def beside(ref, r, n, both=True):
    lane = lanes(n)
    first, last = lane == 0, lane == COLS - 1
    c0, c1 = ref[0, r : r + n, :], ref[1, r : r + n, :]
    e0, e1 = pltpu.roll(c0, COLS - 1, 1), pltpu.roll(c1, COLS - 1, 1)
    w0, w1 = pltpu.roll(c0, 1, 1), pltpu.roll(c1, 1, 1)
    out = [
        (
            c0,
            jnp.where(last, e1, e0),
            jnp.where(first, w1, w0),
            ref[0, r + 1 : r + 1 + n, :],
            ref[0, r - 1 : r - 1 + n, :],
        )
    ]
    if both:
        out.append(
            (
                c1,
                jnp.where(last, e0, e1),
                jnp.where(first, w0, w1),
                ref[1, r + 1 : r + 1 + n, :],
                ref[1, r - 1 : r - 1 + n, :],
            )
        )
    return out


def west_of(ref, r, n):
    first = lanes(n) == 0
    c0, c1 = ref[0, r : r + n, :], ref[1, r : r + n, :]
    w0, w1 = pltpu.roll(c0, 1, 1), pltpu.roll(c1, 1, 1)
    return (c0, jnp.where(first, w1, w0)), (c1, jnp.where(first, w0, w1))


def eights(x):
    return jnp.sum(x.reshape(x.shape[0] // 8, 8, COLS), axis=0)


def coefficients(sums):
    m = [sums[0], sums[1]]
    for k in range(2, 8):
        m.append(2.0 * sums[k] - m[k % 2])
    g = [[0.5 * (m[i + j] + m[abs(i - j)]) for j in range(5) if i + j < 8] for i in range(4)]

    def image(i, j):
        if j == 0:
            return g[i][1]
        return 0.5 * (g[i][j + 1] + g[i][j - 1])

    a = [[g[i][j] - image(i, j) for j in range(i + 1)] for i in range(4)]
    low = [[None] * 4 for _ in range(4)]
    inv, piv = [], []
    for j in range(4):
        pivot = a[j][j]
        for k in range(j):
            pivot = pivot - low[j][k] * low[j][k] * piv[k]
        good = pivot > 1e-6 * a[j][j]
        piv.append(jnp.where(good, pivot, 0.0))
        inv.append(jnp.where(good, 1.0 / jnp.where(good, pivot, 1.0), 0.0))
        for i in range(j + 1, 4):
            s = a[i][j]
            for k in range(j):
                s = s - low[i][k] * low[j][k] * piv[k]
            low[i][j] = s * inv[j]
    y = []
    for i in range(4):
        s = m[i]
        for k in range(i):
            s = s - low[i][k] * y[k]
        y.append(s)
    c = [None] * 4
    for i in reversed(range(4)):
        s = y[i] * inv[i]
        for k in range(i + 1, 4):
            s = s - low[k][i] * c[k]
        c[i] = s
    return c


def ocean_kernel(
    u_hbm, v_hbm, t_hbm, p_hbm, depth_hbm, helm_hbm, land_hbm, clinic_hbm, tropic_hbm,
    u_out, v_out, t_out, p_out,
    uvt, pold, depth, land, cmap, tmap, act, dom,
    ext, pack, pack_t, got_t, got, corner,
    rim, rim_t, rim_got, rim_m, rim_back, edge, edge_got,
    face, rdiag, gain, diag, flow, basis, part,
    in_sem, send_sem, recv_sem, rsend_sem, rrecv_sem, *red,
):
    gx, gy = lax.axis_index("gx"), lax.axis_index("gy")
    east, west = lax.rem(gx + 1, NX_DEV), lax.rem(gx + NX_DEV - 1, NX_DEV)
    north, south = lax.rem(gy + 1, NY_DEV), lax.rem(gy + NY_DEV - 1, NY_DEV)
    own = pl.ds(OFF, ROWS)

    loads = [
        pltpu.make_async_copy(u_hbm, uvt.at[0:4, 8 : 8 + ROWS, :], in_sem.at[0]),
        pltpu.make_async_copy(v_hbm, uvt.at[4:8, 8 : 8 + ROWS, :], in_sem.at[1]),
        pltpu.make_async_copy(p_hbm, pold, in_sem.at[2]),
        pltpu.make_async_copy(depth_hbm, depth, in_sem.at[3]),
        pltpu.make_async_copy(land_hbm, land, in_sem.at[4]),
        pltpu.make_async_copy(clinic_hbm, cmap, in_sem.at[5]),
        pltpu.make_async_copy(tropic_hbm, tmap, in_sem.at[6]),
        pltpu.make_async_copy(helm_hbm, ext.at[HELM, 0, OFF : OFF + ROWS, :], in_sem.at[7]),
        pltpu.make_async_copy(t_hbm, uvt.at[8:12, 8 : 8 + ROWS, :], in_sem.at[8]),
    ]
    for load in loads:
        load.start()

    barrier = pltpu.get_barrier_semaphore()
    greeted = []
    for kind in RED_STAGES if RED_STAGES == ("all",) else RED_STAGES + ("halo",):
        greeted += peers(kind)
    for peer in greeted:
        pl.semaphore_signal(barrier, inc=1, device_id=peer, device_id_type=MESH)

    pack[ROWS:, :] = jnp.zeros((pack.shape[0] - ROWS, COLS), F32)
    for load in loads[:8]:
        load.wait()

    shape = (NX_DEV, NBY)
    mine = lax.broadcasted_iota(jnp.int32, shape, 0) == gx
    shape = (BLOCKS, NBY)
    wanted = lax.broadcasted_iota(jnp.int32, shape, 1) == lax.broadcasted_iota(jnp.int32, shape, 0) + gy * BLOCKS

    def per_block(flags):
        line = jnp.sum(jnp.where(mine, flags, 0.0), axis=0, keepdims=True)
        column = jnp.sum(jnp.where(wanted, line, 0.0), axis=1, keepdims=True)
        return jnp.broadcast_to(column, (BLOCKS, COLS))

    act[...] = per_block(cmap[...].astype(F32))
    dom[...] = per_block(jnp.where(tmap[...] >= 0, 1.0, 0.0))

    def coriolis(b):
        row = lax.broadcasted_iota(jnp.int32, (BY, COLS), 0) + (gy * ROWS + b * BY)
        return 0.2 + 0.6 * ((row.astype(F32) + 0.5) / NY)

    group = lanes(BY) // 16
    for b in range(BLOCKS):
        r = b * BY
        rows = slice(r, r + BY)
        solve = land[rows, :].astype(F32) * dom[b : b + 1, :]
        wet = depth[rows, :] * solve
        u = [uvt[k, 8 + r : 8 + r + BY, :] for k in range(LEVELS)]
        v = [uvt[LEVELS + k, 8 + r : 8 + r + BY, :] for k in range(LEVELS)]
        u_bar = sum(THICK[k] * u[k] for k in range(LEVELS))
        v_bar = sum(THICK[k] * v[k] for k in range(LEVELS))
        cor = 0.2 * coriolis(b)
        mix = 0.1 * (THICK[1] - THICK[0])
        u_hat = u_bar + mix * (u[0] - u[3]) + cor * v_bar
        v_hat = v_bar + mix * (v[0] - v[3]) - cor * u_bar
        fields = [wet, ext[HELM, 0, OFF + r : OFF + r + BY, :], solve * pold[rows, :], u_bar, u_hat, v_bar, v_hat]
        packed = None
        for f, value in enumerate(fields):
            if f != HELM:
                ext[f, 0, OFF + r : OFF + r + BY, :] = value
            moved = pltpu.roll(value, 8 + 16 * f, 1)
            packed = moved if packed is None else jnp.where(group == f, moved, packed)
        pack[rows, :] = packed
    for c in range(3):
        pack_t[:, :, :, 128 * c : 128 * (c + 1)] = pack[128 * c : 128 * (c + 1), :].T.reshape(8, 2, 8, COLS)

    def send(src, dst, k, to):
        copy = pltpu.make_async_remote_copy(
            src_ref=src, dst_ref=dst, send_sem=send_sem.at[k], recv_sem=recv_sem.at[k], device_id=to, device_id_type=MESH
        )
        copy.start()
        return copy

    pl.semaphore_wait(barrier, len(greeted))
    halo = [
        send(pack_t.at[0:7, 0], got_t.at[0:7, 0], 0, (east, gy)),
        send(pack_t.at[0:7, 1], got_t.at[0:7, 1], 1, (west, gy)),
        send(ext.at[:, 0, OFF + ROWS - 8 : OFF + ROWS, :], ext.at[:, 0, LOW:OFF, :], 2, (gx, north)),
        send(ext.at[:, 0, OFF : OFF + 8, :], ext.at[:, 0, OFF + ROWS : HIGH, :], 3, (gx, south)),
        send(pack.at[ROWS - 8 : ROWS, :], corner.at[0], 4, (east, north)),
        send(pack.at[ROWS - 8 : ROWS, :], corner.at[1], 5, (west, north)),
        send(pack.at[0:8, :], corner.at[2], 6, (east, south)),
        send(pack.at[0:8, :], corner.at[3], 7, (west, south)),
    ]

    loads[8].wait()
    pair = lanes(BY) // 2
    for b in range(BLOCKS):
        r = b * BY
        packed = None
        for q in range(PLANES):
            moved = pltpu.roll(uvt[q, 8 + r : 8 + r + BY, :], 2 * q + 1, 1)
            packed = moved if packed is None else jnp.where(pair == q, moved, packed)
        rim[r : r + BY, :] = packed
    rim[ROWS:, :] = jnp.zeros((rim.shape[0] - ROWS, COLS), F32)
    for c in range(3):
        rim_t[:, 128 * c : 128 * (c + 1)] = rim[128 * c : 128 * (c + 1), :].T[: 2 * PLANES, :]
    for q in range(PLANES):
        edge[0, q : q + 1, :] = uvt[q, 8 : 9, :]
        edge[1, q : q + 1, :] = uvt[q, 7 + ROWS : 8 + ROWS, :]
    outer = [
        send(rim_t, rim_got.at[0], 8, (east, gy)),
        send(rim_t, rim_got.at[1], 9, (west, gy)),
        send(edge.at[1], edge_got.at[0], 10, (gx, north)),
        send(edge.at[0], edge_got.at[1], 11, (gx, south)),
    ]

    for copy in halo:
        copy.wait_recv()
    low_half = lax.rem(lanes(8), 16) < 8
    got[0:8, :] = jnp.where(low_half, corner[0], corner[1])
    for c in range(3):
        block = got_t[:, :, :, 128 * c : 128 * (c + 1)].reshape(128, 128).T
        n = min(128, ROWS - 128 * c)
        got[8 + 128 * c : 8 + 128 * c + n, :] = block[:n, :]
    got[8 + ROWS : 16 + ROWS, :] = jnp.where(low_half, corner[2], corner[3])

    chunks = [(r, STEP) for r in range(LOW, HIGH, STEP)]
    lane = lanes(STEP)
    sides = (lane < 8) | (lane >= COLS - 8)
    for r, n in chunks:
        packed = got[r - LOW : r - LOW + n, :]
        for f in range(FIELDS):
            moved = pltpu.roll(packed, COLS - (16 * f + 8), 1)
            ext[f, 1, r : r + n, :] = jnp.where(sides, moved, 1.0 if f == HELM else 0.0)

    for r, n in chunks:
        at = slice(r, r + n)
        for t, (c, e, w, nn, s) in enumerate(beside(ext.at[WET], r, n)):
            four = [jnp.minimum(c, o) for o in (e, w, nn, s)]
            total = ext[HELM, t, at, :] + four[0] + four[1] + four[2] + four[3]
            inverse = 1.0 / total
            rdiag[t, at, :] = inverse
            if t == 0:
                diag[at, :] = total
            for k in range(4):
                face[k, t, at, :] = four[k]
                gain[k, t, at, :] = four[k] * inverse
    for k, (bar, hat) in enumerate(((UB, UH), (VB, VH))):
        for r, n in chunks:
            at = slice(r, r + n)
            for t, (c, *others) in enumerate(beside(ext.at[bar], r, n)):
                spread = sum(face[i, t, at, :] * (o - c) for i, o in enumerate(others))
                flow[k, t, at, :] = ext[WET, t, at, :] * (ext[hat, t, at, :] + 0.1 * spread)

    def image(t, at, others):
        return sum(gain[i, t, at, :] * o for i, o in enumerate(others))

    for r, n in chunks:
        at = slice(r, r + n)
        x = beside(ext.at[X0], r, n)
        for t, (ef, efw) in enumerate(west_of(flow.at[0], r, n)):
            nf, nfs = flow[1, t, at, :], flow[1, t, r - 1 : r - 1 + n, :]
            force = jnp.where(ext[WET, t, at, :] > 0.0, (efw - ef) + (nfs - nf), 0.0)
            c, *others = x[t]
            basis[0, t, at, :] = force * rdiag[t, at, :] + (image(t, at, others) - c)
    for k in range(3):
        for r, n in chunks:
            at = slice(r, r + n)
            for t, (c, *others) in enumerate(beside(basis.at[k], r, n)):
                value = image(t, at, others)
                if k:
                    value = 2.0 * value - basis[k - 1, t, at, :]
                basis[k + 1, t, at, :] = value
    sums = [jnp.zeros((8, COLS), F32) for _ in range(8)]
    for b in range(BLOCKS):
        r = OFF + b * BY
        at = slice(r, r + BY)
        ((c, *others),) = beside(basis.at[3], r, BY, both=False)
        t4 = 2.0 * image(0, at, others) - basis[2, 0, at, :]
        vectors = [basis[k, 0, at, :] for k in range(3)] + [c, t4]
        for k in range(4):
            weighted = diag[at, :] * vectors[k]
            sums[2 * k] = sums[2 * k] + eights(weighted * vectors[k])
            sums[2 * k + 1] = sums[2 * k + 1] + eights(weighted * vectors[k + 1])

    rows8 = lax.broadcasted_iota(jnp.int32, (8, COLS), 0)
    mat = jnp.zeros((8, COLS), F32)
    for k in range(8):
        mat = jnp.where(rows8 == k, jnp.sum(sums[k], axis=0, keepdims=True), mat)
    total = jnp.broadcast_to(jnp.sum(mat, axis=1, keepdims=True), (8, COLS))
    row = jnp.sum(jnp.where(lanes(8) == rows8, total, 0.0), axis=0, keepdims=True)

    def level_updates():
        for copy in outer:
            copy.wait_recv()
        even = lax.rem(lax.broadcasted_iota(jnp.int32, (2 * PLANES, COLS), 0), 2) == 0
        for c in range(3):
            cols = slice(128 * c, 128 * (c + 1))
            from_w, from_e = rim_got[0, :, cols], rim_got[1, :, cols]
            up, down = pltpu.roll(from_e, 2 * PLANES - 1, 0), pltpu.roll(from_w, 1, 0)
            rim_m[0 : 2 * PLANES, :] = jnp.where(even, up, down)
            rim_back[128 * c : 128 * (c + 1), :] = rim_m[...].T
        for q in range(PLANES):
            uvt[q, 7:8, :] = edge_got[0, q : q + 1, :]
            uvt[q, 8 + ROWS : 9 + ROWS, :] = edge_got[1, q : q + 1, :]
        first, last = lanes(BY) == 0, lanes(BY) == COLS - 1

        for b in range(BLOCKS):
            r = b * BY
            rows = slice(r, r + BY)
            at = slice(OFF + r, OFF + r + BY)
            on = act[b : b + 1, :]
            ocean = land[rows, :].astype(F32)
            keep = on * ocean
            off = 1.0 - on
            cor = coriolis(b)
            faces = [face[k, 0, at, :] for k in range(4)]
            rim_row = rim_back[rows, :]

            def around(q):
                c = uvt[q, 8 + r : 8 + r + BY, :]
                side = pltpu.roll(rim_row, COLS - 1 - 2 * q, 1)
                e = jnp.where(last, side, pltpu.roll(c, COLS - 1, 1))
                w = jnp.where(first, side, pltpu.roll(c, 1, 1))
                return c, e, w, uvt[q, 9 + r : 9 + r + BY, :], uvt[q, 7 + r : 7 + r + BY, :]

            def raw(q0):
                out, keepers = [], []
                for k in range(LEVELS):
                    c, *others = around(q0 + k)
                    spread = sum(faces[i] * (o - c) for i, o in enumerate(others))
                    mix = jnp.zeros_like(c)
                    if k < LEVELS - 1:
                        mix = mix + (uvt[q0 + k + 1, 8 + r : 8 + r + BY, :] - c)
                    if k > 0:
                        mix = mix - (c - uvt[q0 + k - 1, 8 + r : 8 + r + BY, :])
                    out.append((c, 0.5 * mix + 0.5 * spread, others))
                return out

            for k, (c, tend, _) in enumerate(raw(0)):
                star = c + 0.2 * (tend + cor * uvt[LEVELS + k, 8 + r : 8 + r + BY, :])
                u_out[k, rows, :] = keep * star + off * c
            for k, (c, tend, _) in enumerate(raw(LEVELS)):
                star = c + 0.2 * (tend - cor * uvt[k, 8 + r : 8 + r + BY, :])
                v_out[k, rows, :] = keep * star + off * c
            for k, (c, tend, (e, w, nn, s)) in enumerate(raw(2 * LEVELS)):
                uk = uvt[k, 8 + r : 8 + r + BY, :]
                vk = uvt[LEVELS + k, 8 + r : 8 + r + BY, :]
                star = c + 0.2 * (tend - 0.5 * (uk * (e - w) + vk * (nn - s)))
                t_out[k, rows, :] = keep * star + off * c

    for s, kind in enumerate(RED_STAGES):
        landing = red[s]
        part[s] = row
        for j, peer in enumerate(peers(kind)):
            pltpu.make_async_remote_copy(
                src_ref=part.at[s], dst_ref=landing.at[j], send_sem=rsend_sem.at[s], recv_sem=rrecv_sem.at[s],
                device_id=peer, device_id_type=MESH,
            ).start()
        if s == 0:
            level_updates()
        every = pltpu.make_async_remote_copy(
            src_ref=landing, dst_ref=landing, send_sem=rsend_sem.at[s], recv_sem=rrecv_sem.at[s],
            device_id=(east, gy), device_id_type=MESH,
        )
        every.wait_recv()
        row = row + jnp.sum(landing[...], axis=0)

    c = coefficients([jnp.broadcast_to(row[:, k : k + 1], (1, COLS)) for k in range(8)])

    def answer(t, at):
        x = ext[X0, t, at, :]
        for k in range(4):
            x = x + c[k] * basis[k, t, at, :]
        return x

    for b in range(BLOCKS):
        rows = slice(b * BY, (b + 1) * BY)
        at = slice(OFF + b * BY, OFF + (b + 1) * BY)
        x0, x1 = answer(0, at), answer(1, at)
        up = answer(0, slice(at.start + 1, at.stop + 1))
        right = jnp.where(lanes(BY) == COLS - 1, pltpu.roll(x1, COLS - 1, 1), pltpu.roll(x0, COLS - 1, 1))
        keep = act[b : b + 1, :] * land[rows, :].astype(F32)
        p_out[rows, :] = x0
        grad_x, grad_y = keep * (right - x0), keep * (up - x0)
        for k in range(LEVELS):
            u_out[k, rows, :] = u_out[k, rows, :] - grad_x
            v_out[k, rows, :] = v_out[k, rows, :] - grad_y

    for copy in halo + outer:
        copy.wait_send()
    for s in range(len(RED_STAGES)):
        pltpu.make_async_remote_copy(
            src_ref=red[s], dst_ref=red[s], send_sem=rsend_sem.at[s], recv_sem=rrecv_sem.at[s],
            device_id=(east, gy), device_id_type=MESH,
        ).wait_send()


def emit_kernel(*refs):
    n = (len(refs) - 1) // 2
    sem = refs[-1]
    copies = [pltpu.make_async_copy(refs[i], refs[n + i], sem.at[i]) for i in range(n)]
    for copy in copies:
        copy.start()
    for copy in copies:
        copy.wait()


def on_device(*args):
    args = args[:7] + (args[7].T, args[8].T)
    vmem, hbm = pltpu.VMEM, pltpu.HBM
    three = jax.ShapeDtypeStruct((LEVELS, ROWS, COLS), F32)
    two = jax.ShapeDtypeStruct((ROWS, COLS), F32)
    shapes = (three, three, three, two)
    tiles = (2, EXT_ROWS, COLS)
    scratch = [
        vmem((PLANES, ROWS + 16, COLS), F32),
        vmem((ROWS, COLS), F32),
        vmem((ROWS, COLS), F32),
        vmem((ROWS, COLS), jnp.int32),
        vmem((NX_DEV, NBY), jnp.int32),
        vmem((NX_DEV, NBY), jnp.int32),
        vmem((BLOCKS, COLS), F32),
        vmem((BLOCKS, COLS), F32),
        vmem((FIELDS,) + tiles, F32),
        vmem((384, COLS), F32),
        vmem((8, 2, 8, 384), F32),
        vmem((8, 2, 8, 384), F32),
        vmem((ROWS + 16, COLS), F32),
        vmem((4, 8, COLS), F32),
        vmem((384, COLS), F32),
        vmem((2 * PLANES, 384), F32),
        vmem((2, 2 * PLANES, 384), F32),
        vmem((COLS, COLS), F32),
        vmem((384, COLS), F32),
        vmem((2, 16, COLS), F32),
        vmem((2, 16, COLS), F32),
        vmem((4,) + tiles, F32),
        vmem(tiles, F32),
        vmem((4,) + tiles, F32),
        vmem((EXT_ROWS, COLS), F32),
        vmem((2,) + tiles, F32),
        vmem((4,) + tiles, F32),
        vmem((len(RED_STAGES), 1, COLS), F32),
        pltpu.SemaphoreType.DMA((9,)),
        pltpu.SemaphoreType.DMA((12,)),
        pltpu.SemaphoreType.DMA((12,)),
        pltpu.SemaphoreType.DMA((len(RED_STAGES),)),
        pltpu.SemaphoreType.DMA((len(RED_STAGES),)),
    ] + [vmem((COUNT[kind], 1, COLS), F32) for kind in RED_STAGES]
    out = pl.pallas_call(
        ocean_kernel,
        out_shape=shapes,
        in_specs=[pl.BlockSpec(memory_space=hbm)] * 9,
        out_specs=[pl.BlockSpec(memory_space=vmem)] * 4,
        scratch_shapes=scratch,
        compiler_params=pltpu.CompilerParams(
            collective_id=0, has_side_effects=True, vmem_limit_bytes=VMEM_LIMIT
        ),
        name="ocean",
    )(*args)
    return pl.pallas_call(
        emit_kernel,
        out_shape=shapes,
        in_specs=[pl.BlockSpec(memory_space=vmem)] * 4,
        out_specs=[pl.BlockSpec(memory_space=hbm)] * 4,
        scratch_shapes=[pltpu.SemaphoreType.DMA((4,))],
        compiler_params=pltpu.CompilerParams(vmem_limit_bytes=8 * 1024 * 1024),
        name="emit",
    )(*out)


def solution(mesh):
    wide, flat = P(None, "gy", "gx"), P("gy", "gx")
    return jax.shard_map(
        on_device,
        mesh=mesh,
        in_specs=(wide, wide, wide, flat, flat, flat, flat, P(), P()),
        out_specs=(wide, wide, wide, flat),
        check_vma=False,
    )
```

time: 267 us -> 31.9 us (0.12)
  blocking collectives: 135 us -> 0 us
  other arithmetic: 38.9 us -> 0 us
  starting transfers between devices: 37.3 us -> 0 us
  Pallas kernels: 0 us -> 26.8 us
  local copies, waits for them, and re-layouts: 30.2 us -> 4.17 us
  between operations: 14.8 us -> 0.65 us
  waiting for transfers between devices: 9.27 us -> 0 us
    psum x16 -> x0, blocking collectives: 135 us -> none  [one_axis_at_a_time(): x = lax.psum(x, axis)]
    ppermute x27 -> x0, starting transfers between devices: 37.3 us -> none  [the longest x11 16.2 us: padded_3(): lax.ppermute(last, axis, up)]
    pallas_call x0 -> x2, Pallas kernels: none -> 26.8 us  [the longest x1 25.5 us: on_device(): pl.pallas_call(ocean_kernel, out_shape=shapes, in_specs=[pl.BlockSpec(mem...]
    reduce_sum x5 -> x0, other arithmetic: 15.8 us -> none  [the longest x1 8.32 us: on_device(): east_flow = wet_cycle * jnp.sum(thick * u_star, 0)]
    slice x18 -> x0, local copies, waits for them, and re-layouts: 12.3 us -> none  [the longest x4 6.02 us: on_device(): inner_faces = tuple((face[1:-1, 1:-1] for face in cycle_faces))]
    unnamed x69 -> x8, local copies, waits for them, and re-layouts: 14.5 us -> 4.17 us
    ppermute x27 -> x0, waiting for transfers between devices: 9.27 us -> none  [the longest x12 6.65 us: padded_3(): lax.ppermute(first, axis, [(b, a) for a, b in up])]
    add x4 -> x0, other arithmetic: 8.4 us -> none  [the longest x1 4.37 us: on_device(): t_new = keep_mask * tracer_raw + (1.0 - active) * tracer]
  transfers between devices with their start and end apart: 27 -> 0, of which waited for: 7 -> 0; matrix products, arithmetic and copies ran while one was open for 14% -> 0% of each run, Pallas kernels for 0% -> 0%
where the time goes in v1:
time: 31.9 us; the launch traced here: 31.6 us
  Pallas kernels  26.8 us (84%)
  local copies, waits for them, and re-layouts  4.17 us (13%)
  between operations  0.65 us (2%)
    pallas_call x1, Pallas kernels, on_device(): pl.pallas_call(ocean_kernel, out_shape=shapes, in_specs=[pl.BlockSpec(mem...  25.5 us
    unnamed x8, local copies, waits for them, and re-layouts  4.17 us
    pallas_call x1, Pallas kernels, on_device(): pl.pallas_call(emit_kernel, out_shape=shapes, in_specs=[pl.BlockSpec(memo...  1.35 us

profile of v1, /device:TPU:1, one launch (start us, length us, event | category | flops | bytes accessed | tf_op | source)
XLA Modules:
  0.0 31.6 jit_solution(11613823535231760519)
XLA Ops:
  0.6 25.5 %ocean.1 = (f32[4,320,128]{2,1,0:T(8,128)}, f32[4,320,128]{2,1,0:T(8,128)}, f32[4,320,128]{2,1,0:T(8,128)}, f32[320,128]{1,0:T(8,128)}) custom-call(f32[4,320,128]{2,1,0:T(8,128)} %u_hbm.1, f32[4,320,128]{2,1,0:T(8,128)} %v_hbm.1, f32[4,320,128]{2,1,0:T(8,128)} %t_hbm.1, f32[320,128]{1,0:T(8,128)} %p_hbm.1, f32[320,128]{1,0:T(8,128)} %depth_hbm.1, ...), custom_call_target="tpu_custom_call" | custom-call | tf_op jit(solution)/shard_map/ocean/pallas_call | solution.py:500
  26.1 0.0 copy-start
  26.1 1.1 %copy-done = f32[4,320,128]{2,1,0:T(8,128)S(1)} copy-done((f32[4,320,128]{2,1,0:T(8,128)S(1)}, f32[4,320,128]{2,1,0:T(8,128)}, u32[]{:S(2)}) %copy-start) | copy-done | bytes 655384
  27.2 0.0 copy-start.1
  27.2 1.1 %copy-done.1 = f32[4,320,128]{2,1,0:T(8,128)S(1)} copy-done((f32[4,320,128]{2,1,0:T(8,128)S(1)}, f32[4,320,128]{2,1,0:T(8,128)}, u32[]{:S(2)}) %copy-start.1) | copy-done | bytes 655384
  28.3 0.0 copy-start.2
  28.3 1.1 %copy-done.2 = f32[4,320,128]{2,1,0:T(8,128)S(1)} copy-done((f32[4,320,128]{2,1,0:T(8,128)S(1)}, f32[4,320,128]{2,1,0:T(8,128)}, u32[]{:S(2)}) %copy-start.2) | copy-done | bytes 655384
  29.4 0.0 copy-start.3
  29.4 0.9 %copy-done.3 = f32[320,128]{1,0:T(8,128)S(1)} copy-done((f32[320,128]{1,0:T(8,128)S(1)}, f32[320,128]{1,0:T(8,128)}, u32[]{:S(2)}) %copy-start.3) | copy-done | bytes 163864
  30.3 1.3 %emit.1 = (f32[4,320,128]{2,1,0:T(8,128)}, f32[4,320,128]{2,1,0:T(8,128)}, f32[4,320,128]{2,1,0:T(8,128)}, f32[320,128]{1,0:T(8,128)}) custom-call(f32[4,320,128]{2,1,0:T(8,128)S(1)} %copy-done, f32[4,320,128]{2,1,0:T(8,128)S(1)} %copy-done.1, f32[4,320,128]{2,1,0:T(8,128)S(1)} %copy-done.2, f32[320,128]{1,0:T(8,128)S(1)} %copy-done.3), custom_call_target="tpu_custom_call" | custom-call | tf_op jit(solution)/shard_map/emit/pallas_call | solution.py:511
Async XLA Ops:
  26.1 1.1 %copy-start = (f32[4,320,128]{2,1,0:T(8,128)S(1)}, f32[4,320,128]{2,1,0:T(8,128)}, u32[]{:S(2)}) copy-start(f32[4,320,128]{2,1,0:T(8,128)} %get-tuple-element.8.refs_0_) | copy-start | bytes 1966084
  27.2 1.1 %copy-start.1 = (f32[4,320,128]{2,1,0:T(8,128)S(1)}, f32[4,320,128]{2,1,0:T(8,128)}, u32[]{:S(2)}) copy-start(f32[4,320,128]{2,1,0:T(8,128)} %get-tuple-element.9.refs_1_) | copy-start | bytes 1966084
  28.3 1.1 %copy-start.2 = (f32[4,320,128]{2,1,0:T(8,128)S(1)}, f32[4,320,128]{2,1,0:T(8,128)}, u32[]{:S(2)}) copy-start(f32[4,320,128]{2,1,0:T(8,128)} %get-tuple-element.10.refs_2_) | copy-start | bytes 1966084
  29.4 0.9 %copy-start.3 = (f32[320,128]{1,0:T(8,128)S(1)}, f32[320,128]{1,0:T(8,128)}, u32[]{:S(2)}) copy-start(f32[320,128]{1,0:T(8,128)} %get-tuple-element.11.refs_3_) | copy-start | bytes 491524

commit v2 on v1

--- a/solution.py
+++ b/solution.py
@@ -23,7 +23,7 @@
 PLANES = 3 * LEVELS
 NX_DEV, NY_DEV = 16, 8
 
-VMEM_LIMIT = 54 * 1024 * 1024
+VMEM_LIMIT = 24 * 1024 * 1024
 RED_STAGES = ("all",)
 
 
@@ -457,6 +457,7 @@
 
 def on_device(*args):
     args = args[:7] + (args[7].T, args[8].T)
+    args = [pltpu.with_memory_space_constraint(x, pltpu.HBM) for x in args]
     vmem, hbm = pltpu.VMEM, pltpu.HBM
     three = jax.ShapeDtypeStruct((LEVELS, ROWS, COLS), F32)
     two = jax.ShapeDtypeStruct((ROWS, COLS), F32)
@@ -499,7 +500,7 @@
     ] + [vmem((COUNT[kind], 1, COLS), F32) for kind in RED_STAGES]
     out = pl.pallas_call(
         ocean_kernel,
-        out_shape=shapes,
+        out_shape=[vmem(x.shape, x.dtype) for x in shapes],
         in_specs=[pl.BlockSpec(memory_space=hbm)] * 9,
         out_specs=[pl.BlockSpec(memory_space=vmem)] * 4,
         scratch_shapes=scratch,

time: 31.9 us -> 26.3 us (0.82)
  local copies, waits for them, and re-layouts: 4.17 us -> 0 us
  Pallas kernels: 26.8 us -> 25.5 us
    unnamed x8 -> x0, local copies, waits for them, and re-layouts: 4.17 us -> none
    pallas_call x1, Pallas kernels: 25.5 us -> 24.1 us  [on_device(): pl.pallas_call(ocean_kernel, out_shape=[vmem(x.shape, x.dtype) for x in s...]
where the time goes in v2:
time: 26.3 us; the launch traced here: 26.1 us
  Pallas kernels  25.5 us (97%)
  between operations  0.64 us (2%)
    pallas_call x1, Pallas kernels, on_device(): pl.pallas_call(ocean_kernel, out_shape=[vmem(x.shape, x.dtype) for x in s...  24.1 us
    pallas_call x1, Pallas kernels, on_device(): pl.pallas_call(emit_kernel, out_shape=shapes, in_specs=[pl.BlockSpec(memo...  1.35 us

profile of v2, /device:TPU:1, one launch (start us, length us, event | category | flops | bytes accessed | tf_op | source)
XLA Modules:
  0.0 26.1 jit_solution(15598512535325487803)
XLA Ops:
  0.6 24.1 %ocean.1 = (f32[4,320,128]{2,1,0:T(8,128)S(1)}, f32[4,320,128]{2,1,0:T(8,128)S(1)}, f32[4,320,128]{2,1,0:T(8,128)S(1)}, f32[320,128]{1,0:T(8,128)S(1)}) custom-call(f32[4,320,128]{2,1,0:T(8,128)} %u_hbm.1, f32[4,320,128]{2,1,0:T(8,128)} %v_hbm.1, f32[4,320,128]{2,1,0:T(8,128)} %t_hbm.1, f32[320,128]{1,0:T(8,128)} %p_hbm.1, f32[320,128]{1,0:T(8,128)} %depth_hbm.1, ...), custom_call_target="tpu_custom_call" | custom-call | tf_op jit(solution)/shard_map/ocean/pallas_call | solution.py:501
  24.8 1.4 %emit.1 = (f32[4,320,128]{2,1,0:T(8,128)}, f32[4,320,128]{2,1,0:T(8,128)}, f32[4,320,128]{2,1,0:T(8,128)}, f32[320,128]{1,0:T(8,128)}) custom-call(f32[4,320,128]{2,1,0:T(8,128)S(1)} %get-tuple-element.8.refs_0_, f32[4,320,128]{2,1,0:T(8,128)S(1)} %get-tuple-element.9.refs_1_, f32[4,320,128]{2,1,0:T(8,128)S(1)} %get-tuple-element.10.refs_2_, ...), custom_call_target="tpu_custom_call" | custom-call | tf_op jit(solution)/shard_map/emit/pallas_call | solution.py:512

commit v3 on v2

--- a/solution.py
+++ b/solution.py
@@ -35,6 +35,16 @@
             for i in (0, 1, NX_DEV - 1)
             for j in (0, 1, NY_DEV - 1)
             if i or j
+        ]
+    if kind == "ball":
+        z, y, x, core = gx // 4, lax.rem(gx, 4), gy // 2, lax.rem(gy, 2)
+        return [
+            (lax.rem(z + i, 4) * 4 + lax.rem(y + j, 4), lax.rem(x + k, 4) * 2 + lax.rem(core + c, 2))
+            for i in (0, 1, 3)
+            for j in (0, 1, 3)
+            for k in (0, 1, 3)
+            for c in (0, 1)
+            if i or j or k or c
         ]
     if kind == "plane":
         base = gx // 4 * 4
@@ -148,7 +158,7 @@
     ext, pack, pack_t, got_t, got, corner,
     rim, rim_t, rim_got, rim_m, rim_back, edge, edge_got,
     face, rdiag, gain, diag, flow, basis, part,
-    in_sem, send_sem, recv_sem, rsend_sem, rrecv_sem, *red,
+    in_sem, send_sem, recv_sem, rsend_sem, rrecv_sem, known, *red,
 ):
     gx, gy = lax.axis_index("gx"), lax.axis_index("gy")
     east, west = lax.rem(gx + 1, NX_DEV), lax.rem(gx + NX_DEV - 1, NX_DEV)
@@ -170,9 +180,7 @@
         load.start()
 
     barrier = pltpu.get_barrier_semaphore()
-    greeted = []
-    for kind in RED_STAGES if RED_STAGES == ("all",) else RED_STAGES + ("halo",):
-        greeted += peers(kind)
+    greeted = peers("ball")
     for peer in greeted:
         pl.semaphore_signal(barrier, inc=1, device_id=peer, device_id_type=MESH)
 
@@ -230,6 +238,8 @@
         return copy
 
     pl.semaphore_wait(barrier, len(greeted))
+    for peer in greeted:
+        pl.semaphore_signal(known, inc=1, device_id=peer, device_id_type=MESH)
     halo = [
         send(pack_t.at[0:7, 0], got_t.at[0:7, 0], 0, (east, gy)),
         send(pack_t.at[0:7, 1], got_t.at[0:7, 1], 1, (west, gy)),
@@ -398,6 +408,7 @@
                 star = c + 0.2 * (tend - 0.5 * (uk * (e - w) + vk * (nn - s)))
                 t_out[k, rows, :] = keep * star + off * c
 
+    pl.semaphore_wait(known, len(greeted))
     for s, kind in enumerate(RED_STAGES):
         landing = red[s]
         part[s] = row
@@ -497,6 +508,7 @@
         pltpu.SemaphoreType.DMA((12,)),
         pltpu.SemaphoreType.DMA((len(RED_STAGES),)),
         pltpu.SemaphoreType.DMA((len(RED_STAGES),)),
+        pltpu.SemaphoreType.REGULAR,
     ] + [vmem((COUNT[kind], 1, COLS), F32) for kind in RED_STAGES]
     out = pl.pallas_call(
         ocean_kernel,

time: 26.3 us -> 26.3 us (level)
  no operation moved by 1% of the time
where the time goes in v3:
time: 26.3 us; the launch traced here: 26.1 us
  Pallas kernels  25.5 us (97%)
  between operations  0.64 us (2%)
    pallas_call x1, Pallas kernels, on_device(): pl.pallas_call(ocean_kernel, out_shape=[vmem(x.shape, x.dtype) for x in s...  24.1 us
    pallas_call x1, Pallas kernels, on_device(): pl.pallas_call(emit_kernel, out_shape=shapes, in_specs=[pl.BlockSpec(memo...  1.35 us

profile of v3, /device:TPU:1, one launch (start us, length us, event | category | flops | bytes accessed | tf_op | source)
XLA Modules:
  0.0 26.1 jit_solution(15032277892383469867)
XLA Ops:
  0.6 24.1 %ocean.1 = (f32[4,320,128]{2,1,0:T(8,128)S(1)}, f32[4,320,128]{2,1,0:T(8,128)S(1)}, f32[4,320,128]{2,1,0:T(8,128)S(1)}, f32[320,128]{1,0:T(8,128)S(1)}) custom-call(f32[4,320,128]{2,1,0:T(8,128)} %u_hbm.1, f32[4,320,128]{2,1,0:T(8,128)} %v_hbm.1, f32[4,320,128]{2,1,0:T(8,128)} %t_hbm.1, f32[320,128]{1,0:T(8,128)} %p_hbm.1, f32[320,128]{1,0:T(8,128)} %depth_hbm.1, ...), custom_call_target="tpu_custom_call" | custom-call | tf_op jit(solution)/shard_map/ocean/pallas_call | solution.py:513
  24.8 1.4 %emit.1 = (f32[4,320,128]{2,1,0:T(8,128)}, f32[4,320,128]{2,1,0:T(8,128)}, f32[4,320,128]{2,1,0:T(8,128)}, f32[320,128]{1,0:T(8,128)}) custom-call(f32[4,320,128]{2,1,0:T(8,128)S(1)} %get-tuple-element.8.refs_0_, f32[4,320,128]{2,1,0:T(8,128)S(1)} %get-tuple-element.9.refs_1_, f32[4,320,128]{2,1,0:T(8,128)S(1)} %get-tuple-element.10.refs_2_, ...), custom_call_target="tpu_custom_call" | custom-call | tf_op jit(solution)/shard_map/emit/pallas_call | solution.py:524

commit v4 on v2

--- a/solution.py
+++ b/solution.py
@@ -24,6 +24,9 @@
 NX_DEV, NY_DEV = 16, 8
 
 VMEM_LIMIT = 24 * 1024 * 1024
+TO_EAST = (6, 4, 5, 6, 5, 5, 4)
+TO_WEST = (5, 4, 5, 5, 4, 5, 4)
+EAST_ROWS, WEST_ROWS = 40, 32
 RED_STAGES = ("all",)
 
 
@@ -51,6 +54,18 @@
         for i in range(NX_DEV)
         for j in range(NY_DEV)
         if i or j
+    ]
+
+
+def nearby(step):
+    gx, gy = lax.axis_index("gx"), lax.axis_index("gy")
+    z, y, core = gx // 4, lax.rem(gx, 4), lax.rem(gy, 2)
+    return [
+        (lax.rem(z + i, 4) * 4 + lax.rem(y + j, 4), gy + 2 * step if c == 0 else gy + 2 * step + 1 - 2 * core)
+        for i in (0, 1, 3)
+        for j in (0, 1, 3)
+        for c in (0, 1)
+        if i or j or c or step
     ]
 
 
@@ -145,10 +160,10 @@
     u_hbm, v_hbm, t_hbm, p_hbm, depth_hbm, helm_hbm, land_hbm, clinic_hbm, tropic_hbm,
     u_out, v_out, t_out, p_out,
     uvt, pold, depth, land, cmap, tmap, act, dom,
-    ext, pack, pack_t, got_t, got, corner,
+    ext, pack, pack_t, for_e, for_w, from_w, from_e, got_t, got, corner,
     rim, rim_t, rim_got, rim_m, rim_back, edge, edge_got,
     face, rdiag, gain, diag, flow, basis, part,
-    in_sem, send_sem, recv_sem, rsend_sem, rrecv_sem, *red,
+    in_sem, send_sem, recv_sem, rsend_sem, rrecv_sem, known, far, *red,
 ):
     gx, gy = lax.axis_index("gx"), lax.axis_index("gy")
     east, west = lax.rem(gx + 1, NX_DEV), lax.rem(gx + NX_DEV - 1, NX_DEV)
@@ -170,11 +185,23 @@
         load.start()
 
     barrier = pltpu.get_barrier_semaphore()
-    greeted = []
-    for kind in RED_STAGES if RED_STAGES == ("all",) else RED_STAGES + ("halo",):
-        greeted += peers(kind)
-    for peer in greeted:
-        pl.semaphore_signal(barrier, inc=1, device_id=peer, device_id_type=MESH)
+    has_n, has_s = gy < NY_DEV - 1, gy > 0
+    up_x, down_x = gy < NY_DEV - 2, gy > 1
+
+    def greet(sem):
+        for step, there in ((0, None), (1, up_x), (-1, down_x)):
+
+            def tell(step=step):
+                for peer in nearby(step):
+                    pl.semaphore_signal(sem, inc=1, device_id=peer, device_id_type=MESH)
+
+            tell() if there is None else pl.when(there)(tell)
+
+    def hear(sem):
+        inner = lax.rem((gy // 2 + 1) // 2, 2)
+        pl.semaphore_wait(sem, 35 + 18 * inner)
+
+    greet(barrier)
 
     pack[ROWS:, :] = jnp.zeros((pack.shape[0] - ROWS, COLS), F32)
     for load in loads[:8]:
@@ -220,26 +247,49 @@
             packed = moved if packed is None else jnp.where(group == f, moved, packed)
         pack[rows, :] = packed
     for c in range(3):
-        pack_t[:, :, :, 128 * c : 128 * (c + 1)] = pack[128 * c : 128 * (c + 1), :].T.reshape(8, 2, 8, COLS)
-
-    def send(src, dst, k, to):
-        copy = pltpu.make_async_remote_copy(
-            src_ref=src, dst_ref=dst, send_sem=send_sem.at[k], recv_sem=recv_sem.at[k], device_id=to, device_id_type=MESH
-        )
-        copy.start()
-        return copy
-
-    pl.semaphore_wait(barrier, len(greeted))
-    halo = [
-        send(pack_t.at[0:7, 0], got_t.at[0:7, 0], 0, (east, gy)),
-        send(pack_t.at[0:7, 1], got_t.at[0:7, 1], 1, (west, gy)),
-        send(ext.at[:, 0, OFF + ROWS - 8 : OFF + ROWS, :], ext.at[:, 0, LOW:OFF, :], 2, (gx, north)),
-        send(ext.at[:, 0, OFF : OFF + 8, :], ext.at[:, 0, OFF + ROWS : HIGH, :], 3, (gx, south)),
-        send(pack.at[ROWS - 8 : ROWS, :], corner.at[0], 4, (east, north)),
-        send(pack.at[ROWS - 8 : ROWS, :], corner.at[1], 5, (west, north)),
-        send(pack.at[0:8, :], corner.at[2], 6, (east, south)),
-        send(pack.at[0:8, :], corner.at[3], 7, (west, south)),
-    ]
+        cols = slice(128 * c, 128 * (c + 1))
+        pack_t[...] = pack[cols, :].T
+        at_e = at_w = 0
+        for f in range(FIELDS):
+            ne, nw = TO_EAST[f], TO_WEST[f]
+            for_e[at_e : at_e + ne, cols] = pack_t[16 * f + 8 - ne : 16 * f + 8, :]
+            for_w[at_w : at_w + nw, cols] = pack_t[16 * f + 8 : 16 * f + 8 + nw, :]
+            at_e, at_w = at_e + ne, at_w + nw
+
+    routes = {
+        0: (for_e, from_w, (east, gy), None),
+        1: (for_w, from_e, (west, gy), None),
+        2: (ext.at[:, 0, OFF + ROWS - 8 : OFF + ROWS, :], ext.at[:, 0, LOW:OFF, :], (gx, north), "n"),
+        3: (ext.at[:, 0, OFF : OFF + 8, :], ext.at[:, 0, OFF + ROWS : HIGH, :], (gx, south), "s"),
+        4: (pack.at[ROWS - 8 : ROWS, :], corner.at[0], (east, north), "n"),
+        5: (pack.at[ROWS - 8 : ROWS, :], corner.at[1], (west, north), "n"),
+        6: (pack.at[0:8, :], corner.at[2], (east, south), "s"),
+        7: (pack.at[0:8, :], corner.at[3], (west, south), "s"),
+        8: (rim_t, rim_got.at[0], (east, gy), None),
+        9: (rim_t, rim_got.at[1], (west, gy), None),
+        10: (edge.at[1], edge_got.at[0], (gx, north), "n"),
+        11: (edge.at[0], edge_got.at[1], (gx, south), "s"),
+    }
+    HALO, OUTER = range(8), range(8, 12)
+
+    def transfer(which, what):
+        def go(keys):
+            for k in keys:
+                src, dst, to, _ = routes[k]
+                copy = pltpu.make_async_remote_copy(
+                    src_ref=src, dst_ref=dst, send_sem=send_sem.at[k], recv_sem=recv_sem.at[k],
+                    device_id=to, device_id_type=MESH,
+                )
+                getattr(copy, what)()
+
+        go([k for k in which if routes[k][3] is None])
+        for way, other in (("n", "s"), ("s", "n")):
+            there = {"n": has_n, "s": has_s}[other if what == "wait_recv" else way]
+            pl.when(there)(functools.partial(go, [k for k in which if routes[k][3] == way]))
+
+    hear(barrier)
+    greet(known)
+    transfer(HALO, "start")
 
     loads[8].wait()
     pair = lanes(BY) // 2
@@ -256,31 +306,50 @@
     for q in range(PLANES):
         edge[0, q : q + 1, :] = uvt[q, 8 : 9, :]
         edge[1, q : q + 1, :] = uvt[q, 7 + ROWS : 8 + ROWS, :]
-    outer = [
-        send(rim_t, rim_got.at[0], 8, (east, gy)),
-        send(rim_t, rim_got.at[1], 9, (west, gy)),
-        send(edge.at[1], edge_got.at[0], 10, (gx, north)),
-        send(edge.at[0], edge_got.at[1], 11, (gx, south)),
-    ]
-
-    for copy in halo:
-        copy.wait_recv()
+    transfer(OUTER, "start")
+    transfer(HALO, "wait_recv")
+    hear(known)
+
+    @pl.when((gy // 2 == 1) | (gy // 2 == 2))
+    def _():
+        pl.semaphore_signal(
+            far, inc=1, device_id=(gx, gy + 4 * lax.rem(gy // 2 - 1, 2) - 2), device_id_type=MESH
+        )
+
     low_half = lax.rem(lanes(8), 16) < 8
-    got[0:8, :] = jnp.where(low_half, corner[0], corner[1])
+    nothing = jnp.where(lanes(8) // 16 == HELM, 1.0, 0.0)
     for c in range(3):
-        block = got_t[:, :, :, 128 * c : 128 * (c + 1)].reshape(128, 128).T
+        cols = slice(128 * c, 128 * (c + 1))
+        at_w = at_e = 0
+        for f in range(FIELDS):
+            nw, ne = TO_EAST[f], TO_WEST[f]
+            got_t[16 * f + 8 - nw : 16 * f + 8, :] = from_w[at_w : at_w + nw, cols]
+            got_t[16 * f + 8 : 16 * f + 8 + ne, :] = from_e[at_e : at_e + ne, cols]
+            at_w, at_e = at_w + nw, at_e + ne
+        block = got_t[...].T
         n = min(128, ROWS - 128 * c)
         got[8 + 128 * c : 8 + 128 * c + n, :] = block[:n, :]
-    got[8 + ROWS : 16 + ROWS, :] = jnp.where(low_half, corner[2], corner[3])
+    for k, there, first, halo_at in ((0, has_s, 0, LOW), (2, has_n, 8 + ROWS, OFF + ROWS)):
+
+        @pl.when(there)
+        def _(k=k, first=first):
+            got[first : first + 8, :] = jnp.where(low_half, corner[k], corner[k + 1])
+
+        @pl.when(jnp.logical_not(there))
+        def _(k=k, first=first, halo_at=halo_at):
+            got[first : first + 8, :] = nothing
+            edge_got[k // 2] = jnp.zeros((16, COLS), F32)
+            for f in range(FIELDS):
+                ext[f, 0, halo_at : halo_at + 8, :] = jnp.full((8, COLS), 1.0 if f == HELM else 0.0, F32)
 
     chunks = [(r, STEP) for r in range(LOW, HIGH, STEP)]
     lane = lanes(STEP)
-    sides = (lane < 8) | (lane >= COLS - 8)
     for r, n in chunks:
         packed = got[r - LOW : r - LOW + n, :]
         for f in range(FIELDS):
             moved = pltpu.roll(packed, COLS - (16 * f + 8), 1)
-            ext[f, 1, r : r + n, :] = jnp.where(sides, moved, 1.0 if f == HELM else 0.0)
+            came = (lane < TO_WEST[f]) | (lane >= COLS - TO_EAST[f])
+            ext[f, 1, r : r + n, :] = jnp.where(came, moved, 1.0 if f == HELM else 0.0)
 
     for r, n in chunks:
         at = slice(r, r + n)
@@ -340,8 +409,7 @@
     row = jnp.sum(jnp.where(lanes(8) == rows8, total, 0.0), axis=0, keepdims=True)
 
     def level_updates():
-        for copy in outer:
-            copy.wait_recv()
+        transfer(OUTER, "wait_recv")
         even = lax.rem(lax.broadcasted_iota(jnp.int32, (2 * PLANES, COLS), 0), 2) == 0
         for c in range(3):
             cols = slice(128 * c, 128 * (c + 1))
@@ -397,6 +465,10 @@
                 vk = uvt[LEVELS + k, 8 + r : 8 + r + BY, :]
                 star = c + 0.2 * (tend - 0.5 * (uk * (e - w) + vk * (nn - s)))
                 t_out[k, rows, :] = keep * star + off * c
+
+    @pl.when((gy // 2 == 0) | (gy // 2 == 3))
+    def _():
+        pl.semaphore_wait(far, 1)
 
     for s, kind in enumerate(RED_STAGES):
         landing = red[s]
@@ -436,8 +508,7 @@
             u_out[k, rows, :] = u_out[k, rows, :] - grad_x
             v_out[k, rows, :] = v_out[k, rows, :] - grad_y
 
-    for copy in halo + outer:
-        copy.wait_send()
+    transfer(range(12), "wait_send")
     for s in range(len(RED_STAGES)):
         pltpu.make_async_remote_copy(
             src_ref=red[s], dst_ref=red[s], send_sem=rsend_sem.at[s], recv_sem=rrecv_sem.at[s],
@@ -474,8 +545,12 @@
         vmem((BLOCKS, COLS), F32),
         vmem((FIELDS,) + tiles, F32),
         vmem((384, COLS), F32),
-        vmem((8, 2, 8, 384), F32),
-        vmem((8, 2, 8, 384), F32),
+        vmem((COLS, COLS), F32),
+        vmem((EAST_ROWS, 384), F32),
+        vmem((WEST_ROWS, 384), F32),
+        vmem((EAST_ROWS, 384), F32),
+        vmem((WEST_ROWS, 384), F32),
+        vmem((COLS, COLS), F32),
         vmem((ROWS + 16, COLS), F32),
         vmem((4, 8, COLS), F32),
         vmem((384, COLS), F32),
@@ -497,6 +572,8 @@
         pltpu.SemaphoreType.DMA((12,)),
         pltpu.SemaphoreType.DMA((len(RED_STAGES),)),
         pltpu.SemaphoreType.DMA((len(RED_STAGES),)),
+        pltpu.SemaphoreType.REGULAR,
+        pltpu.SemaphoreType.REGULAR,
     ] + [vmem((COUNT[kind], 1, COLS), F32) for kind in RED_STAGES]
     out = pl.pallas_call(
         ocean_kernel,

time: 26.3 us -> 25.4 us (0.966)
  Pallas kernels: 25.5 us -> 24.7 us
    pallas_call x1, Pallas kernels: 24.1 us -> 23.3 us  [on_device(): pl.pallas_call(ocean_kernel, out_shape=[vmem(x.shape, x.dtype) for x in s...]
where the time goes in v4:
time: 25.4 us; the launch traced here: 25.3 us
  Pallas kernels  24.7 us (97%)
  between operations  0.64 us (3%)
    pallas_call x1, Pallas kernels, on_device(): pl.pallas_call(ocean_kernel, out_shape=[vmem(x.shape, x.dtype) for x in s...  23.3 us
    pallas_call x1, Pallas kernels, on_device(): pl.pallas_call(emit_kernel, out_shape=shapes, in_specs=[pl.BlockSpec(memo...  1.35 us

profile of v4, /device:TPU:1, one launch (start us, length us, event | category | flops | bytes accessed | tf_op | source)
XLA Modules:
  0.0 25.3 jit_solution(6053885599226945969)
XLA Ops:
  0.6 23.3 %ocean.1 = (f32[4,320,128]{2,1,0:T(8,128)S(1)}, f32[4,320,128]{2,1,0:T(8,128)S(1)}, f32[4,320,128]{2,1,0:T(8,128)S(1)}, f32[320,128]{1,0:T(8,128)S(1)}) custom-call(f32[4,320,128]{2,1,0:T(8,128)} %u_hbm.1, f32[4,320,128]{2,1,0:T(8,128)} %v_hbm.1, f32[4,320,128]{2,1,0:T(8,128)} %t_hbm.1, f32[320,128]{1,0:T(8,128)} %p_hbm.1, f32[320,128]{1,0:T(8,128)} %depth_hbm.1, ...), custom_call_target="tpu_custom_call" | custom-call | tf_op jit(solution)/shard_map/ocean/pallas_call | solution.py:578
  24.0 1.4 %emit.1 = (f32[4,320,128]{2,1,0:T(8,128)}, f32[4,320,128]{2,1,0:T(8,128)}, f32[4,320,128]{2,1,0:T(8,128)}, f32[320,128]{1,0:T(8,128)}) custom-call(f32[4,320,128]{2,1,0:T(8,128)S(1)} %get-tuple-element.8.refs_0_, f32[4,320,128]{2,1,0:T(8,128)S(1)} %get-tuple-element.9.refs_1_, f32[4,320,128]{2,1,0:T(8,128)S(1)} %get-tuple-element.10.refs_2_, ...), custom_call_target="tpu_custom_call" | custom-call | tf_op jit(solution)/shard_map/emit/pallas_call | solution.py:589

commit v5 on v4

--- a/solution.py
+++ b/solution.py
@@ -27,6 +27,8 @@
 TO_EAST = (6, 4, 5, 6, 5, 5, 4)
 TO_WEST = (5, 4, 5, 5, 4, 5, 4)
 EAST_ROWS, WEST_ROWS = 40, 32
+EMIT = 80
+HALVES = ((20, 24), (16, 16))
 RED_STAGES = ("all",)
 
 
@@ -158,11 +160,11 @@
 
 def ocean_kernel(
     u_hbm, v_hbm, t_hbm, p_hbm, depth_hbm, helm_hbm, land_hbm, clinic_hbm, tropic_hbm,
-    u_out, v_out, t_out, p_out,
+    u_out, v_out, t_out, basis, guess, kept, sums_out,
     uvt, pold, depth, land, cmap, tmap, act, dom,
-    ext, pack, pack_t, for_e, for_w, from_w, from_e, got_t, got, corner,
+    ext, pack, pack_t, for_e, for_w, from_w, from_e, tail, got_t, got, corner,
     rim, rim_t, rim_got, rim_m, rim_back, edge, edge_got,
-    face, rdiag, gain, diag, flow, basis, part,
+    face, rdiag, gain, diag, flow, part,
     in_sem, send_sem, recv_sem, rsend_sem, rrecv_sem, known, far, *red,
 ):
     gx, gy = lax.axis_index("gx"), lax.axis_index("gy")
@@ -247,14 +249,18 @@
             packed = moved if packed is None else jnp.where(group == f, moved, packed)
         pack[rows, :] = packed
     for c in range(3):
-        cols = slice(128 * c, 128 * (c + 1))
-        pack_t[...] = pack[cols, :].T
-        at_e = at_w = 0
+        pack_t[...] = pack[128 * c : 128 * (c + 1), :].T
+        e_ref, w_ref = (tail.at[0], tail.at[1]) if c == 2 else (for_e, for_w)
+        at_e, at_w = (0, 0) if c == 2 else (EAST_ROWS * c, WEST_ROWS * c)
         for f in range(FIELDS):
             ne, nw = TO_EAST[f], TO_WEST[f]
-            for_e[at_e : at_e + ne, cols] = pack_t[16 * f + 8 - ne : 16 * f + 8, :]
-            for_w[at_w : at_w + nw, cols] = pack_t[16 * f + 8 : 16 * f + 8 + nw, :]
+            e_ref[at_e : at_e + ne, :] = pack_t[16 * f + 8 - ne : 16 * f + 8, :]
+            w_ref[at_w : at_w + nw, :] = pack_t[16 * f + 8 : 16 * f + 8 + nw, :]
             at_e, at_w = at_e + ne, at_w + nw
+    for i, (ref, whole) in enumerate(((for_e, EAST_ROWS), (for_w, WEST_ROWS))):
+        half, size = HALVES[i]
+        moved = pltpu.roll(tail[i, half : half + size, :], COLS // 2, 1)
+        ref[2 * whole :, :] = jnp.where(lanes(size) < COLS // 2, tail[i, 0:size, :], moved)
 
     routes = {
         0: (for_e, from_w, (east, gy), None),
@@ -288,8 +294,9 @@
             pl.when(there)(functools.partial(go, [k for k in which if routes[k][3] == way]))
 
     hear(barrier)
+    transfer((0, 1), "start")
     greet(known)
-    transfer(HALO, "start")
+    transfer(HALO[2:], "start")
 
     loads[8].wait()
     pair = lanes(BY) // 2
@@ -318,13 +325,18 @@
 
     low_half = lax.rem(lanes(8), 16) < 8
     nothing = jnp.where(lanes(8) // 16 == HELM, 1.0, 0.0)
+    for i, (ref, whole) in enumerate(((from_w, EAST_ROWS), (from_e, WEST_ROWS))):
+        half, size = HALVES[i]
+        shared = ref[2 * whole :, :]
+        tail[i, 0:size, :] = shared
+        tail[i, half : half + size, :] = pltpu.roll(shared, COLS // 2, 1)
     for c in range(3):
-        cols = slice(128 * c, 128 * (c + 1))
-        at_w = at_e = 0
+        w_ref, e_ref = (tail.at[0], tail.at[1]) if c == 2 else (from_w, from_e)
+        at_w, at_e = (0, 0) if c == 2 else (EAST_ROWS * c, WEST_ROWS * c)
         for f in range(FIELDS):
             nw, ne = TO_EAST[f], TO_WEST[f]
-            got_t[16 * f + 8 - nw : 16 * f + 8, :] = from_w[at_w : at_w + nw, cols]
-            got_t[16 * f + 8 : 16 * f + 8 + ne, :] = from_e[at_e : at_e + ne, cols]
+            got_t[16 * f + 8 - nw : 16 * f + 8, :] = w_ref[at_w : at_w + nw, :]
+            got_t[16 * f + 8 : 16 * f + 8 + ne, :] = e_ref[at_e : at_e + ne, :]
             at_w, at_e = at_w + nw, at_e + ne
         block = got_t[...].T
         n = min(128, ROWS - 128 * c)
@@ -380,6 +392,7 @@
             nf, nfs = flow[1, t, at, :], flow[1, t, r - 1 : r - 1 + n, :]
             force = jnp.where(ext[WET, t, at, :] > 0.0, (efw - ef) + (nfs - nf), 0.0)
             c, *others = x[t]
+            guess[t, at, :] = c
             basis[0, t, at, :] = force * rdiag[t, at, :] + (image(t, at, others) - c)
     for k in range(3):
         for r, n in chunks:
@@ -393,13 +406,19 @@
     for b in range(BLOCKS):
         r = OFF + b * BY
         at = slice(r, r + BY)
-        ((c, *others),) = beside(basis.at[3], r, BY, both=False)
-        t4 = 2.0 * image(0, at, others) - basis[2, 0, at, :]
-        vectors = [basis[k, 0, at, :] for k in range(3)] + [c, t4]
+        vectors = [basis[k, 0, at, :] for k in range(4)]
+        c = vectors[3]
+        right = jnp.where(
+            lanes(BY) == COLS - 1, pltpu.roll(basis[3, 1, at, :], COLS - 1, 1), pltpu.roll(c, COLS - 1, 1)
+        )
+        up = basis[3, 0, r + 1 : r + 1 + BY, :]
         for k in range(4):
             weighted = diag[at, :] * vectors[k]
             sums[2 * k] = sums[2 * k] + eights(weighted * vectors[k])
-            sums[2 * k + 1] = sums[2 * k + 1] + eights(weighted * vectors[k + 1])
+            if k < 3:
+                sums[2 * k + 1] = sums[2 * k + 1] + eights(weighted * vectors[k + 1])
+        sums[7] = sums[7] + eights(c * (face[0, 0, at, :] * right + face[2, 0, at, :] * up))
+    sums[7] = 4.0 * sums[7] - sums[5]
 
     rows8 = lax.broadcasted_iota(jnp.int32, (8, COLS), 0)
     mat = jnp.zeros((8, COLS), F32)
@@ -429,6 +448,7 @@
             on = act[b : b + 1, :]
             ocean = land[rows, :].astype(F32)
             keep = on * ocean
+            kept[rows, :] = keep
             off = 1.0 - on
             cor = coriolis(b)
             faces = [face[k, 0, at, :] for k in range(4)]
@@ -487,27 +507,7 @@
         every.wait_recv()
         row = row + jnp.sum(landing[...], axis=0)
 
-    c = coefficients([jnp.broadcast_to(row[:, k : k + 1], (1, COLS)) for k in range(8)])
-
-    def answer(t, at):
-        x = ext[X0, t, at, :]
-        for k in range(4):
-            x = x + c[k] * basis[k, t, at, :]
-        return x
-
-    for b in range(BLOCKS):
-        rows = slice(b * BY, (b + 1) * BY)
-        at = slice(OFF + b * BY, OFF + (b + 1) * BY)
-        x0, x1 = answer(0, at), answer(1, at)
-        up = answer(0, slice(at.start + 1, at.stop + 1))
-        right = jnp.where(lanes(BY) == COLS - 1, pltpu.roll(x1, COLS - 1, 1), pltpu.roll(x0, COLS - 1, 1))
-        keep = act[b : b + 1, :] * land[rows, :].astype(F32)
-        p_out[rows, :] = x0
-        grad_x, grad_y = keep * (right - x0), keep * (up - x0)
-        for k in range(LEVELS):
-            u_out[k, rows, :] = u_out[k, rows, :] - grad_x
-            v_out[k, rows, :] = v_out[k, rows, :] - grad_y
-
+    sums_out[...] = row
     transfer(range(12), "wait_send")
     for s in range(len(RED_STAGES)):
         pltpu.make_async_remote_copy(
@@ -516,12 +516,41 @@
         ).wait_send()
 
 
-def emit_kernel(*refs):
-    n = (len(refs) - 1) // 2
-    sem = refs[-1]
-    copies = [pltpu.make_async_copy(refs[i], refs[n + i], sem.at[i]) for i in range(n)]
-    for copy in copies:
-        copy.start()
+def emit_kernel(u_ref, v_ref, t_ref, basis, guess, kept, sums, u_hbm, v_hbm, t_hbm, p_hbm, u_new, v_new, p_new, sem):
+    copies = [pltpu.make_async_copy(t_ref, t_hbm, sem.at[0])]
+    copies[0].start()
+    row = sums[...]
+    c = coefficients([jnp.broadcast_to(row[:, k : k + 1], (1, COLS)) for k in range(8)])
+
+    def answer(t, at):
+        x = guess[t, at, :]
+        for k in range(4):
+            x = x + c[k] * basis[k, t, at, :]
+        return x
+
+    last = lanes(EMIT) == COLS - 1
+    for b in range(ROWS // EMIT):
+        rows = slice(b * EMIT, (b + 1) * EMIT)
+        at = slice(OFF + rows.start, OFF + rows.stop)
+        x0, x1 = answer(0, at), answer(1, at)
+        up = answer(0, slice(at.start + 1, at.stop + 1))
+        right = jnp.where(last, pltpu.roll(x1, COLS - 1, 1), pltpu.roll(x0, COLS - 1, 1))
+        keep = kept[rows, :]
+        p_new[rows, :] = x0
+        grad_x, grad_y = keep * (right - x0), keep * (up - x0)
+        for k in range(LEVELS):
+            u_new[k, rows, :] = u_ref[k, rows, :] - grad_x
+            v_new[k, rows, :] = v_ref[k, rows, :] - grad_y
+        for i, (src, dst) in enumerate(
+            (
+                (u_new.at[:, rows, :], u_hbm.at[:, rows, :]),
+                (v_new.at[:, rows, :], v_hbm.at[:, rows, :]),
+                (p_new.at[rows, :], p_hbm.at[rows, :]),
+            )
+        ):
+            copy = pltpu.make_async_copy(src, dst, sem.at[1 + 3 * b + i])
+            copy.start()
+            copies.append(copy)
     for copy in copies:
         copy.wait()
 
@@ -546,10 +575,11 @@
         vmem((FIELDS,) + tiles, F32),
         vmem((384, COLS), F32),
         vmem((COLS, COLS), F32),
-        vmem((EAST_ROWS, 384), F32),
-        vmem((WEST_ROWS, 384), F32),
-        vmem((EAST_ROWS, 384), F32),
-        vmem((WEST_ROWS, 384), F32),
+        vmem((2 * EAST_ROWS + HALVES[0][1], COLS), F32),
+        vmem((2 * WEST_ROWS + HALVES[1][1], COLS), F32),
+        vmem((2 * EAST_ROWS + HALVES[0][1], COLS), F32),
+        vmem((2 * WEST_ROWS + HALVES[1][1], COLS), F32),
+        vmem((2, 48, COLS), F32),
         vmem((COLS, COLS), F32),
         vmem((ROWS + 16, COLS), F32),
         vmem((4, 8, COLS), F32),
@@ -565,7 +595,6 @@
         vmem((4,) + tiles, F32),
         vmem((EXT_ROWS, COLS), F32),
         vmem((2,) + tiles, F32),
-        vmem((4,) + tiles, F32),
         vmem((len(RED_STAGES), 1, COLS), F32),
         pltpu.SemaphoreType.DMA((9,)),
         pltpu.SemaphoreType.DMA((12,)),
@@ -577,9 +606,10 @@
     ] + [vmem((COUNT[kind], 1, COLS), F32) for kind in RED_STAGES]
     out = pl.pallas_call(
         ocean_kernel,
-        out_shape=[vmem(x.shape, x.dtype) for x in shapes],
+        out_shape=[vmem(x.shape, F32) for x in (three, three, three)]
+        + [vmem((4,) + tiles, F32), vmem(tiles, F32), vmem((ROWS, COLS), F32), vmem((1, COLS), F32)],
         in_specs=[pl.BlockSpec(memory_space=hbm)] * 9,
-        out_specs=[pl.BlockSpec(memory_space=vmem)] * 4,
+        out_specs=[pl.BlockSpec(memory_space=vmem)] * 7,
         scratch_shapes=scratch,
         compiler_params=pltpu.CompilerParams(
             collective_id=0, has_side_effects=True, vmem_limit_bytes=VMEM_LIMIT
@@ -589,9 +619,10 @@
     return pl.pallas_call(
         emit_kernel,
         out_shape=shapes,
-        in_specs=[pl.BlockSpec(memory_space=vmem)] * 4,
+        in_specs=[pl.BlockSpec(memory_space=vmem)] * 7,
         out_specs=[pl.BlockSpec(memory_space=hbm)] * 4,
-        scratch_shapes=[pltpu.SemaphoreType.DMA((4,))],
+        scratch_shapes=[vmem(three.shape, F32), vmem(three.shape, F32), vmem(two.shape, F32)]
+        + [pltpu.SemaphoreType.DMA((1 + 3 * (ROWS // EMIT),))],
         compiler_params=pltpu.CompilerParams(vmem_limit_bytes=8 * 1024 * 1024),
         name="emit",
     )(*out)

time: 25.4 us -> 24.7 us (0.972)
  Pallas kernels: 24.7 us -> 23.9 us
    pallas_call x1, Pallas kernels: 23.3 us -> 22.5 us  [on_device(): pl.pallas_call(ocean_kernel, out_shape=[vmem(x.shape, F32) for x in (thre...]
where the time goes in v5:
time: 24.7 us; the launch traced here: 24.6 us
  Pallas kernels  23.9 us (97%)
  between operations  0.64 us (3%)
    pallas_call x1, Pallas kernels, on_device(): pl.pallas_call(ocean_kernel, out_shape=[vmem(x.shape, F32) for x in (thre...  22.5 us
    pallas_call x1, Pallas kernels, on_device(): pl.pallas_call(emit_kernel, out_shape=shapes, in_specs=[pl.BlockSpec(memo...  1.46 us

profile of v5, /device:TPU:1, one launch (start us, length us, event | category | flops | bytes accessed | tf_op | source)
XLA Modules:
  0.0 24.6 jit_solution(14185590675704534367)
XLA Ops:
  0.6 22.5 %ocean.1 = (f32[4,320,128]{2,1,0:T(8,128)S(1)}, f32[4,320,128]{2,1,0:T(8,128)S(1)}, f32[4,320,128]{2,1,0:T(8,128)S(1)}, f32[4,2,352,128]{3,2,1,0:T(8,128)S(1)}, ...) custom-call(f32[4,320,128]{2,1,0:T(8,128)} %u_hbm.1, f32[4,320,128]{2,1,0:T(8,128)} %v_hbm.1, ...), custom_call_target="tpu_custom_call" | custom-call | tf_op jit(solution)/shard_map/ocean/pallas_call | solution.py:607
  23.1 1.5 %emit.1 = (f32[4,320,128]{2,1,0:T(8,128)}, f32[4,320,128]{2,1,0:T(8,128)}, f32[4,320,128]{2,1,0:T(8,128)}, f32[320,128]{1,0:T(8,128)}) custom-call(f32[4,320,128]{2,1,0:T(8,128)S(1)} %get-tuple-element.11.u_ref, f32[4,320,128]{2,1,0:T(8,128)S(1)} %get-tuple-element.12.v_ref, f32[4,320,128]{2,1,0:T(8,128)S(1)} %get-tuple-element.13.t_ref, ...), custom_call_target="tpu_custom_call" | custom-call | tf_op jit(solution)/shard_map/emit/pallas_call | solution.py:619

commit v6 on v5

--- a/solution.py
+++ b/solution.py
@@ -59,13 +59,16 @@
     ]
 
 
-def nearby(step):
+BESIDE = ((0, 1), (1, 1), (0, 3), (3, 3), (0, 0))
+APART = ((1, 0), (3, 0), (1, 3), (3, 1))
+
+
+def nearby(step, ways):
     gx, gy = lax.axis_index("gx"), lax.axis_index("gy")
     z, y, core = gx // 4, lax.rem(gx, 4), lax.rem(gy, 2)
     return [
         (lax.rem(z + i, 4) * 4 + lax.rem(y + j, 4), gy + 2 * step if c == 0 else gy + 2 * step + 1 - 2 * core)
-        for i in (0, 1, 3)
-        for j in (0, 1, 3)
+        for i, j in ways
         for c in (0, 1)
         if i or j or c or step
     ]
@@ -78,32 +81,25 @@
     return lax.broadcasted_iota(jnp.int32, (rows, COLS), 1)
 
 
-def beside(ref, r, n, both=True):
+def beside(ref, r, n, turned=None):
     lane = lanes(n)
     first, last = lane == 0, lane == COLS - 1
     c0, c1 = ref[0, r : r + n, :], ref[1, r : r + n, :]
-    e0, e1 = pltpu.roll(c0, COLS - 1, 1), pltpu.roll(c1, COLS - 1, 1)
-    w0, w1 = pltpu.roll(c0, 1, 1), pltpu.roll(c1, 1, 1)
-    out = [
+    if turned is None:
+        e0, w0 = pltpu.roll(c0, COLS - 1, 1), pltpu.roll(c0, 1, 1)
+    else:
+        e0, w0 = turned[0, r : r + n, :], turned[1, r : r + n, :]
+    e1, w1 = pltpu.roll(c1, COLS - 1, 1), pltpu.roll(c1, 1, 1)
+    return [
         (
-            c0,
-            jnp.where(last, e1, e0),
-            jnp.where(first, w1, w0),
-            ref[0, r + 1 : r + 1 + n, :],
-            ref[0, r - 1 : r - 1 + n, :],
+            c,
+            jnp.where(last, other_e, own_e),
+            jnp.where(first, other_w, own_w),
+            ref[t, r + 1 : r + 1 + n, :],
+            ref[t, r - 1 : r - 1 + n, :],
         )
+        for t, (c, own_e, other_e, own_w, other_w) in enumerate(((c0, e0, e1, w0, w1), (c1, e1, e0, w1, w0)))
     ]
-    if both:
-        out.append(
-            (
-                c1,
-                jnp.where(last, e0, e1),
-                jnp.where(first, w0, w1),
-                ref[1, r + 1 : r + 1 + n, :],
-                ref[1, r - 1 : r - 1 + n, :],
-            )
-        )
-    return out
 
 
 def west_of(ref, r, n):
@@ -164,7 +160,7 @@
     uvt, pold, depth, land, cmap, tmap, act, dom,
     ext, pack, pack_t, for_e, for_w, from_w, from_e, tail, got_t, got, corner,
     rim, rim_t, rim_got, rim_m, rim_back, edge, edge_got,
-    face, rdiag, gain, diag, flow, part,
+    face, rdiag, gain, diag, flow, turned, part,
     in_sem, send_sem, recv_sem, rsend_sem, rrecv_sem, known, far, *red,
 ):
     gx, gy = lax.axis_index("gx"), lax.axis_index("gy")
@@ -183,27 +179,27 @@
         pltpu.make_async_copy(helm_hbm, ext.at[HELM, 0, OFF : OFF + ROWS, :], in_sem.at[7]),
         pltpu.make_async_copy(t_hbm, uvt.at[8:12, 8 : 8 + ROWS, :], in_sem.at[8]),
     ]
-    for load in loads:
-        load.start()
-
     barrier = pltpu.get_barrier_semaphore()
     has_n, has_s = gy < NY_DEV - 1, gy > 0
     up_x, down_x = gy < NY_DEV - 2, gy > 1
 
     def greet(sem):
-        for step, there in ((0, None), (1, up_x), (-1, down_x)):
-
-            def tell(step=step):
-                for peer in nearby(step):
-                    pl.semaphore_signal(sem, inc=1, device_id=peer, device_id_type=MESH)
-
-            tell() if there is None else pl.when(there)(tell)
+        for ways in (BESIDE, APART):
+            for step, there in ((0, None), (1, up_x), (-1, down_x)):
+
+                def tell(step=step, ways=ways):
+                    for peer in nearby(step, ways):
+                        pl.semaphore_signal(sem, inc=1, device_id=peer, device_id_type=MESH)
+
+                tell() if there is None else pl.when(there)(tell)
 
     def hear(sem):
         inner = lax.rem((gy // 2 + 1) // 2, 2)
         pl.semaphore_wait(sem, 35 + 18 * inner)
 
     greet(barrier)
+    for load in loads:
+        load.start()
 
     pack[ROWS:, :] = jnp.zeros((pack.shape[0] - ROWS, COLS), F32)
     for load in loads[:8]:
@@ -314,6 +310,17 @@
         edge[0, q : q + 1, :] = uvt[q, 8 : 9, :]
         edge[1, q : q + 1, :] = uvt[q, 7 + ROWS : 8 + ROWS, :]
     transfer(OUTER, "start")
+
+    def turn(start, size):
+        at = slice(start, start + size)
+        for i, f in enumerate((WET, UB, VB, X0)):
+            value = ext[f, 0, at, :]
+            turned[2 * i, at, :] = pltpu.roll(value, COLS - 1, 1)
+            if f != X0:
+                turned[2 * i + 1, at, :] = pltpu.roll(value, 1, 1)
+
+    for b in range(BLOCKS):
+        turn(OFF + b * BY, BY)
     transfer(HALO, "wait_recv")
     hear(known)
 
@@ -363,9 +370,12 @@
             came = (lane < TO_WEST[f]) | (lane >= COLS - TO_EAST[f])
             ext[f, 1, r : r + n, :] = jnp.where(came, moved, 1.0 if f == HELM else 0.0)
 
+    turn(LOW, 8)
+    turn(OFF + ROWS, 8)
+
     for r, n in chunks:
         at = slice(r, r + n)
-        for t, (c, e, w, nn, s) in enumerate(beside(ext.at[WET], r, n)):
+        for t, (c, e, w, nn, s) in enumerate(beside(ext.at[WET], r, n, turned.at[0:2])):
             four = [jnp.minimum(c, o) for o in (e, w, nn, s)]
             total = ext[HELM, t, at, :] + four[0] + four[1] + four[2] + four[3]
             inverse = 1.0 / total
@@ -375,25 +385,33 @@
             for k in range(4):
                 face[k, t, at, :] = four[k]
                 gain[k, t, at, :] = four[k] * inverse
+    for r, n in chunks:
+        at = slice(r, r + n)
+        last = lanes(n) == COLS - 1
+        x0, x1 = ext[X0, 0, at, :], ext[X0, 1, at, :]
+        e0, e1 = turned[6, at, :], pltpu.roll(x1, COLS - 1, 1)
+        slope_e = jnp.where(last, e1, e0) - x0, jnp.where(last, e0, e1) - x1
+        for t, x in enumerate((x0, x1)):
+            guess[t, at, :] = x
+            slopes = slope_e[t], ext[X0, t, r + 1 : r + 1 + n, :] - x
+            for k, face_at in ((0, 0), (1, 2)):
+                flow[k, t, at, :] = face[face_at, t, at, :] * slopes[k]
     for k, (bar, hat) in enumerate(((UB, UH), (VB, VH))):
         for r, n in chunks:
             at = slice(r, r + n)
-            for t, (c, *others) in enumerate(beside(ext.at[bar], r, n)):
+            for t, (c, *others) in enumerate(beside(ext.at[bar], r, n, turned.at[2 * k + 2 : 2 * k + 4])):
                 spread = sum(face[i, t, at, :] * (o - c) for i, o in enumerate(others))
-                flow[k, t, at, :] = ext[WET, t, at, :] * (ext[hat, t, at, :] + 0.1 * spread)
+                flow[k, t, at, :] = ext[WET, t, at, :] * (ext[hat, t, at, :] + 0.1 * spread) - flow[k, t, at, :]
 
     def image(t, at, others):
         return sum(gain[i, t, at, :] * o for i, o in enumerate(others))
 
     for r, n in chunks:
         at = slice(r, r + n)
-        x = beside(ext.at[X0], r, n)
         for t, (ef, efw) in enumerate(west_of(flow.at[0], r, n)):
             nf, nfs = flow[1, t, at, :], flow[1, t, r - 1 : r - 1 + n, :]
-            force = jnp.where(ext[WET, t, at, :] > 0.0, (efw - ef) + (nfs - nf), 0.0)
-            c, *others = x[t]
-            guess[t, at, :] = c
-            basis[0, t, at, :] = force * rdiag[t, at, :] + (image(t, at, others) - c)
+            residual = (efw - ef) + (nfs - nf) - ext[HELM, t, at, :] * ext[X0, t, at, :]
+            basis[0, t, at, :] = jnp.where(ext[WET, t, at, :] > 0.0, residual * rdiag[t, at, :], 0.0)
     for k in range(3):
         for r, n in chunks:
             at = slice(r, r + n)
@@ -595,6 +613,7 @@
         vmem((4,) + tiles, F32),
         vmem((EXT_ROWS, COLS), F32),
         vmem((2,) + tiles, F32),
+        vmem((7, EXT_ROWS, COLS), F32),
         vmem((len(RED_STAGES), 1, COLS), F32),
         pltpu.SemaphoreType.DMA((9,)),
         pltpu.SemaphoreType.DMA((12,)),

time: 24.7 us -> 24.4 us (0.988)
  Pallas kernels: 23.9 us -> 23.6 us
    pallas_call x1, Pallas kernels: 22.5 us -> 22.1 us  [on_device(): pl.pallas_call(ocean_kernel, out_shape=[vmem(x.shape, F32) for x in (thre...]
where the time goes in v6:
time: 24.4 us; the launch traced here: 24.2 us
  Pallas kernels  23.6 us (97%)
  between operations  0.64 us (3%)
    pallas_call x1, Pallas kernels, on_device(): pl.pallas_call(ocean_kernel, out_shape=[vmem(x.shape, F32) for x in (thre...  22.1 us
    pallas_call x1, Pallas kernels, on_device(): pl.pallas_call(emit_kernel, out_shape=shapes, in_specs=[pl.BlockSpec(memo...  1.46 us

profile of v6, /device:TPU:1, one launch (start us, length us, event | category | flops | bytes accessed | tf_op | source)
XLA Modules:
  0.0 24.2 jit_solution(14856228053252494732)
XLA Ops:
  0.6 22.1 %ocean.1 = (f32[4,320,128]{2,1,0:T(8,128)S(1)}, f32[4,320,128]{2,1,0:T(8,128)S(1)}, f32[4,320,128]{2,1,0:T(8,128)S(1)}, f32[4,2,352,128]{3,2,1,0:T(8,128)S(1)}, ...) custom-call(f32[4,320,128]{2,1,0:T(8,128)} %u_hbm.1, f32[4,320,128]{2,1,0:T(8,128)} %v_hbm.1, ...), custom_call_target="tpu_custom_call" | custom-call | tf_op jit(solution)/shard_map/ocean/pallas_call | solution.py:626
  22.8 1.5 %emit.1 = (f32[4,320,128]{2,1,0:T(8,128)}, f32[4,320,128]{2,1,0:T(8,128)}, f32[4,320,128]{2,1,0:T(8,128)}, f32[320,128]{1,0:T(8,128)}) custom-call(f32[4,320,128]{2,1,0:T(8,128)S(1)} %get-tuple-element.11.u_ref, f32[4,320,128]{2,1,0:T(8,128)S(1)} %get-tuple-element.12.v_ref, f32[4,320,128]{2,1,0:T(8,128)S(1)} %get-tuple-element.13.t_ref, ...), custom_call_target="tpu_custom_call" | custom-call | tf_op jit(solution)/shard_map/emit/pallas_call | solution.py:638

commit v7 on v6

--- a/solution.py
+++ b/solution.py
@@ -27,7 +27,7 @@
 TO_EAST = (6, 4, 5, 6, 5, 5, 4)
 TO_WEST = (5, 4, 5, 5, 4, 5, 4)
 EAST_ROWS, WEST_ROWS = 40, 32
-EMIT = 80
+EMIT = 160
 HALVES = ((20, 24), (16, 16))
 RED_STAGES = ("all",)
 
@@ -290,9 +290,10 @@
             pl.when(there)(functools.partial(go, [k for k in which if routes[k][3] == way]))
 
     hear(barrier)
+    transfer((4, 5, 6, 7), "start")
     transfer((0, 1), "start")
+    transfer((2, 3), "start")
     greet(known)
-    transfer(HALO[2:], "start")
 
     loads[8].wait()
     pair = lanes(BY) // 2
@@ -309,8 +310,6 @@
     for q in range(PLANES):
         edge[0, q : q + 1, :] = uvt[q, 8 : 9, :]
         edge[1, q : q + 1, :] = uvt[q, 7 + ROWS : 8 + ROWS, :]
-    transfer(OUTER, "start")
-
     def turn(start, size):
         at = slice(start, start + size)
         for i, f in enumerate((WET, UB, VB, X0)):
@@ -321,6 +320,8 @@
 
     for b in range(BLOCKS):
         turn(OFF + b * BY, BY)
+    transfer((0, 1), "wait_send")
+    transfer(OUTER, "start")
     transfer(HALO, "wait_recv")
     hear(known)
 
@@ -523,10 +524,13 @@
             device_id=(east, gy), device_id_type=MESH,
         )
         every.wait_recv()
-        row = row + jnp.sum(landing[...], axis=0)
+        parts = [jnp.sum(landing[j : min(j + 16, COUNT[kind])], axis=0) for j in range(0, COUNT[kind], 16)]
+        while len(parts) > 1:
+            parts = [sum(parts[j : j + 2]) for j in range(0, len(parts), 2)]
+        row = row + parts[0]
 
     sums_out[...] = row
-    transfer(range(12), "wait_send")
+    transfer(range(2, 12), "wait_send")
     for s in range(len(RED_STAGES)):
         pltpu.make_async_remote_copy(
             src_ref=red[s], dst_ref=red[s], send_sem=rsend_sem.at[s], recv_sem=rrecv_sem.at[s],

time: 24.4 us -> 24.2 us (level)
  no operation moved by 1% of the time
where the time goes in v7:
time: 24.2 us; the launch traced here: 24.1 us
  Pallas kernels  23.4 us (97%)
  between operations  0.64 us (3%)
    pallas_call x1, Pallas kernels, on_device(): pl.pallas_call(ocean_kernel, out_shape=[vmem(x.shape, F32) for x in (thre...  22 us
    pallas_call x1, Pallas kernels, on_device(): pl.pallas_call(emit_kernel, out_shape=shapes, in_specs=[pl.BlockSpec(memo...  1.44 us

profile of v7, /device:TPU:1, one launch (start us, length us, event | category | flops | bytes accessed | tf_op | source)
XLA Modules:
  0.0 24.1 jit_solution(4366665104748872101)
XLA Ops:
  0.6 22.0 %ocean.1 = (f32[4,320,128]{2,1,0:T(8,128)S(1)}, f32[4,320,128]{2,1,0:T(8,128)S(1)}, f32[4,320,128]{2,1,0:T(8,128)S(1)}, f32[4,2,352,128]{3,2,1,0:T(8,128)S(1)}, ...) custom-call(f32[4,320,128]{2,1,0:T(8,128)} %u_hbm.1, f32[4,320,128]{2,1,0:T(8,128)} %v_hbm.1, ...), custom_call_target="tpu_custom_call" | custom-call | tf_op jit(solution)/shard_map/ocean/pallas_call | solution.py:630
  22.6 1.4 %emit.1 = (f32[4,320,128]{2,1,0:T(8,128)}, f32[4,320,128]{2,1,0:T(8,128)}, f32[4,320,128]{2,1,0:T(8,128)}, f32[320,128]{1,0:T(8,128)}) custom-call(f32[4,320,128]{2,1,0:T(8,128)S(1)} %get-tuple-element.11.u_ref, f32[4,320,128]{2,1,0:T(8,128)S(1)} %get-tuple-element.12.v_ref, f32[4,320,128]{2,1,0:T(8,128)S(1)} %get-tuple-element.13.t_ref, ...), custom_call_target="tpu_custom_call" | custom-call | tf_op jit(solution)/shard_map/emit/pallas_call | solution.py:642

commit v8 on v7

--- a/solution.py
+++ b/solution.py
@@ -222,7 +222,7 @@
         row = lax.broadcasted_iota(jnp.int32, (BY, COLS), 0) + (gy * ROWS + b * BY)
         return 0.2 + 0.6 * ((row.astype(F32) + 0.5) / NY)
 
-    group = lanes(BY) // 16
+    group = (lanes(BY) + 8) // 16
     for b in range(BLOCKS):
         r = b * BY
         rows = slice(r, r + BY)
@@ -241,7 +241,7 @@
         for f, value in enumerate(fields):
             if f != HELM:
                 ext[f, 0, OFF + r : OFF + r + BY, :] = value
-            moved = pltpu.roll(value, 8 + 16 * f, 1)
+            moved = pltpu.roll(value, 16 * f, 1) if f else value
             packed = moved if packed is None else jnp.where(group == f, moved, packed)
         pack[rows, :] = packed
     for c in range(3):
@@ -250,8 +250,8 @@
         at_e, at_w = (0, 0) if c == 2 else (EAST_ROWS * c, WEST_ROWS * c)
         for f in range(FIELDS):
             ne, nw = TO_EAST[f], TO_WEST[f]
-            e_ref[at_e : at_e + ne, :] = pack_t[16 * f + 8 - ne : 16 * f + 8, :]
-            w_ref[at_w : at_w + nw, :] = pack_t[16 * f + 8 : 16 * f + 8 + nw, :]
+            e_ref[at_e : at_e + ne, :] = pack_t[(16 * f - 8) % 128 + 8 - ne : (16 * f - 8) % 128 + 8, :]
+            w_ref[at_w : at_w + nw, :] = pack_t[16 * f : 16 * f + nw, :]
             at_e, at_w = at_e + ne, at_w + nw
     for i, (ref, whole) in enumerate(((for_e, EAST_ROWS), (for_w, WEST_ROWS))):
         half, size = HALVES[i]
@@ -331,8 +331,8 @@
             far, inc=1, device_id=(gx, gy + 4 * lax.rem(gy // 2 - 1, 2) - 2), device_id_type=MESH
         )
 
-    low_half = lax.rem(lanes(8), 16) < 8
-    nothing = jnp.where(lanes(8) // 16 == HELM, 1.0, 0.0)
+    low_half = lax.rem(lanes(8) + 8, 16) < 8
+    nothing = jnp.where((lanes(8) + 8) // 16 == HELM, 1.0, 0.0)
     for i, (ref, whole) in enumerate(((from_w, EAST_ROWS), (from_e, WEST_ROWS))):
         half, size = HALVES[i]
         shared = ref[2 * whole :, :]
@@ -343,8 +343,8 @@
         at_w, at_e = (0, 0) if c == 2 else (EAST_ROWS * c, WEST_ROWS * c)
         for f in range(FIELDS):
             nw, ne = TO_EAST[f], TO_WEST[f]
-            got_t[16 * f + 8 - nw : 16 * f + 8, :] = w_ref[at_w : at_w + nw, :]
-            got_t[16 * f + 8 : 16 * f + 8 + ne, :] = e_ref[at_e : at_e + ne, :]
+            got_t[(16 * f - 8) % 128 + 8 - nw : (16 * f - 8) % 128 + 8, :] = w_ref[at_w : at_w + nw, :]
+            got_t[16 * f : 16 * f + ne, :] = e_ref[at_e : at_e + ne, :]
             at_w, at_e = at_w + nw, at_e + ne
         block = got_t[...].T
         n = min(128, ROWS - 128 * c)
@@ -367,7 +367,7 @@
     for r, n in chunks:
         packed = got[r - LOW : r - LOW + n, :]
         for f in range(FIELDS):
-            moved = pltpu.roll(packed, COLS - (16 * f + 8), 1)
+            moved = pltpu.roll(packed, COLS - 16 * f, 1) if f else packed
             came = (lane < TO_WEST[f]) | (lane >= COLS - TO_EAST[f])
             ext[f, 1, r : r + n, :] = jnp.where(came, moved, 1.0 if f == HELM else 0.0)
 

time: 24.2 us -> 24.1 us (level)
  no operation moved by 1% of the time
where the time goes in v8:
time: 24.1 us; the launch traced here: 24 us
  Pallas kernels  23.4 us (97%)
  between operations  0.64 us (3%)
    pallas_call x1, Pallas kernels, on_device(): pl.pallas_call(ocean_kernel, out_shape=[vmem(x.shape, F32) for x in (thre...  21.9 us
    pallas_call x1, Pallas kernels, on_device(): pl.pallas_call(emit_kernel, out_shape=shapes, in_specs=[pl.BlockSpec(memo...  1.44 us

profile of v8, /device:TPU:1, one launch (start us, length us, event | category | flops | bytes accessed | tf_op | source)
XLA Modules:
  0.0 24.0 jit_solution(2417680786848073267)
XLA Ops:
  0.6 21.9 %ocean.1 = (f32[4,320,128]{2,1,0:T(8,128)S(1)}, f32[4,320,128]{2,1,0:T(8,128)S(1)}, f32[4,320,128]{2,1,0:T(8,128)S(1)}, f32[4,2,352,128]{3,2,1,0:T(8,128)S(1)}, ...) custom-call(f32[4,320,128]{2,1,0:T(8,128)} %u_hbm.1, f32[4,320,128]{2,1,0:T(8,128)} %v_hbm.1, ...), custom_call_target="tpu_custom_call" | custom-call | tf_op jit(solution)/shard_map/ocean/pallas_call | solution.py:630
  22.6 1.4 %emit.1 = (f32[4,320,128]{2,1,0:T(8,128)}, f32[4,320,128]{2,1,0:T(8,128)}, f32[4,320,128]{2,1,0:T(8,128)}, f32[320,128]{1,0:T(8,128)}) custom-call(f32[4,320,128]{2,1,0:T(8,128)S(1)} %get-tuple-element.11.u_ref, f32[4,320,128]{2,1,0:T(8,128)S(1)} %get-tuple-element.12.v_ref, f32[4,320,128]{2,1,0:T(8,128)S(1)} %get-tuple-element.13.t_ref, ...), custom_call_target="tpu_custom_call" | custom-call | tf_op jit(solution)/shard_map/emit/pallas_call | solution.py:642

commit v9 on v8

--- a/solution.py
+++ b/solution.py
@@ -53,7 +53,7 @@
         return [(lax.rem(gx + 4 * j, NX_DEV), gy) for j in range(1, 4)]
     return [
         (lax.rem(gx + i, NX_DEV), lax.rem(gy + j, NY_DEV))
-        for i in range(NX_DEV)
+        for i in (*range(1, NX_DEV), 0)
         for j in range(NY_DEV)
         if i or j
     ]

time: 24.1 us -> 24.1 us (level)
  no operation moved by 1% of the time
where the time goes in v9:
time: 24.1 us; the launch traced here: 24 us
  Pallas kernels  23.3 us (97%)
  between operations  0.64 us (3%)
    pallas_call x1, Pallas kernels, on_device(): pl.pallas_call(ocean_kernel, out_shape=[vmem(x.shape, F32) for x in (thre...  21.9 us
    pallas_call x1, Pallas kernels, on_device(): pl.pallas_call(emit_kernel, out_shape=shapes, in_specs=[pl.BlockSpec(memo...  1.44 us

profile of v9, /device:TPU:1, one launch (start us, length us, event | category | flops | bytes accessed | tf_op | source)
XLA Modules:
  0.0 24.0 jit_solution(4153415117448084336)
XLA Ops:
  0.6 21.9 %ocean.1 = (f32[4,320,128]{2,1,0:T(8,128)S(1)}, f32[4,320,128]{2,1,0:T(8,128)S(1)}, f32[4,320,128]{2,1,0:T(8,128)S(1)}, f32[4,2,352,128]{3,2,1,0:T(8,128)S(1)}, ...) custom-call(f32[4,320,128]{2,1,0:T(8,128)} %u_hbm.1, f32[4,320,128]{2,1,0:T(8,128)} %v_hbm.1, ...), custom_call_target="tpu_custom_call" | custom-call | tf_op jit(solution)/shard_map/ocean/pallas_call | solution.py:630
  22.5 1.4 %emit.1 = (f32[4,320,128]{2,1,0:T(8,128)}, f32[4,320,128]{2,1,0:T(8,128)}, f32[4,320,128]{2,1,0:T(8,128)}, f32[320,128]{1,0:T(8,128)}) custom-call(f32[4,320,128]{2,1,0:T(8,128)S(1)} %get-tuple-element.11.u_ref, f32[4,320,128]{2,1,0:T(8,128)S(1)} %get-tuple-element.12.v_ref, f32[4,320,128]{2,1,0:T(8,128)S(1)} %get-tuple-element.13.t_ref, ...), custom_call_target="tpu_custom_call" | custom-call | tf_op jit(solution)/shard_map/emit/pallas_call | solution.py:642
